TPU v7x, 128 devices: a whole 4x4x4 slice. The times are simulated.
128 devices in a mesh: tile: 8 (over y, core), slab: 16 (over z, x).
Axes of the slice: x: 4, y: 4, z: 4, core: 2. Of those that a mesh axis runs over, the one named last changes fastest.
Arguments:
- volume: float32 [512, 32768], P('slab', 'tile'), may hold values from -6 to 6
- measured: float32 [512, 8192], P('slab', 'tile'), may hold values from -6 to 6
- weights: float32 [512, 8192], P('slab', 'tile'), may hold values from 0.25 to 4
- footprints: float32 [2048, 32, 128], P('tile'), may hold values from -0.1875 to 0.1875
- foot_pixel: int32 [2048], P('tile'), may hold values from 0 to 31
- foot_strip: int32 [2048], P('tile'), may hold values from 0 to 255
Outputs:
- smoothed: float32 [512, 32768], P('slab', 'tile')
- residual: float32 [512, 8192], P('slab', 'tile')
Inputs may be any that keep to these rules, and one draw needn't show every extreme that they name: foot_pixel names one of the 32 pixel blocks of the tile that holds the footprint block. foot_strip names a strip of 32 rays.
All inputs are finite; a program needn't handle non-finite values.
Results may differ from a plain program's by a relative error of at most 0.0003.
Values sent between devices are 32-bit elements; how exact they have to be, the bound alone decides.
No kernel may reach another device: no remote copies, remote signals or barrier semaphores. Data moves between devices by JAX's collectives and lax.ppermute only.
A program may use at most 64 MiB of HBM per device.

v0:
```python
import jax
import jax.numpy as jnp
from jax import lax
from jax.experimental import pallas as pl
from jax.experimental.pallas import tpu as pltpu
from jax.sharding import Mesh
from jax.sharding import PartitionSpec as P

PASSES = 3
TILE = ("tile_0", "tile_1")
SLAB = ("slab_0", "slab_1")
GROUP = 4
UNROLL = 16

huber_width = 0.5
smooth_rate = 0.2


VM = pl.BlockSpec(memory_space=pltpu.VMEM)
SM = pl.BlockSpec(memory_space=pltpu.SMEM)
F32 = jnp.float32
BF16 = jnp.bfloat16


def call(kernel, outs, ins, scratch=(), smem=0, flops=1000000, limit=24):
    return pl.pallas_call(
        kernel,
        out_shape=[jax.ShapeDtypeStruct(s, F32) for s in outs],
        in_specs=[SM] * smem + [VM] * (len(ins) - smem),
        out_specs=[VM] * len(outs),
        scratch_shapes=list(scratch),
        compiler_params=pltpu.CompilerParams(vmem_limit_bytes=limit << 20),
        cost_estimate=pl.CostEstimate(flops=flops, bytes_accessed=1 << 20, transcendentals=0),
    )(*ins)


def halves(value):
    high = value.astype(BF16)
    return high, (value - high.astype(F32)).astype(BF16)


def lane_groups(shape):
    return lax.broadcasted_iota(jnp.int32, shape, 1) // 32


def place(meta, b):
    word = meta[b]
    return word & 63, (word >> 6) & 3, word >> 8


def forward_loop(meta, foot, high, low, rays):
    rays[...] = jnp.zeros_like(rays)
    groups = lane_groups((32, 128))

    def step(g, carry):
        where = [place(meta, GROUP * g + i) for i in range(GROUP)]
        left = jnp.concatenate([jnp.concatenate([high[w[2]], low[w[2]]], axis=1) for w in where], axis=0)
        fh, fl = halves(foot[pl.ds(GROUP * g, GROUP)].reshape(GROUP * 32, 128))
        right = jnp.concatenate(
            [jnp.concatenate([fh, fh], axis=1), jnp.concatenate([fl, jnp.zeros_like(fl)], axis=1)], axis=0
        )
        both = lax.dot_general(left, right, (((1,), (1,)), ((), ())), preferred_element_type=F32)
        product = both[:, :128] + both[:, 128:]
        for i, (entry, spot, _) in enumerate(where):
            own = jnp.where(groups == i, product[32 * i : 32 * i + 32], 0.0)
            rays[entry] += pltpu.roll(own, ((spot - i) & 3) * 32, 1)
        return carry

    lax.fori_loop(0, foot.shape[0] // GROUP, step, 0, unroll=UNROLL)


def back_loop(meta, foot, rays, field):
    field[...] = jnp.zeros_like(field)
    groups = lane_groups((32, 128))

    def step(g, carry):
        where = [place(meta, GROUP * g + i) for i in range(GROUP)]
        rows = []
        for i, (entry, spot, _) in enumerate(where):
            turned = pltpu.roll(rays[entry], ((i - spot) & 3) * 32, 1)
            own = jnp.where(groups == i, turned, 0.0)
            rows.append(jnp.concatenate(halves(own), axis=1))
        left = jnp.concatenate(rows, axis=0)
        fh, fl = halves(foot[pl.ds(GROUP * g, GROUP)].reshape(GROUP * 32, 128))
        right = jnp.concatenate(
            [jnp.concatenate([fh, fl], axis=1), jnp.concatenate([fh, jnp.zeros_like(fl)], axis=1)], axis=0
        )
        both = lax.dot_general(left, right, (((1,), (0,)), ((), ())), preferred_element_type=F32)
        product = both[:, :128] + both[:, 128:]
        for i, (_, _, pixel) in enumerate(where):
            field[pixel] += product[32 * i : 32 * i + 32]
        return carry

    lax.fori_loop(0, foot.shape[0] // GROUP, step, 0, unroll=UNROLL)


def hand_out(rays, mine, theirs):
    mine[...] = rays[:32].reshape(mine.shape)
    theirs[...] = rays[32:].reshape(theirs.shape)


def first_kernel(meta, foot, volume, mine, theirs, high, low, rays):
    for p in range(high.shape[0]):
        high[p], low[p] = halves(volume[:, 128 * p : 128 * p + 128])
    forward_loop(meta, foot, high, low, rays)
    hand_out(rays, mine, theirs)


def folded(value):
    return jnp.sum(value.reshape(-1, 8, 128), axis=0)


def there_and_back(meta, foot, pieces, mine, theirs, field, high, low, rays):
    for slot, piece in enumerate(pieces):
        rays[8 * slot : 8 * slot + 8] = piece[...]
    back_loop(meta, foot, rays, field)
    for p in range(high.shape[0]):
        high[p], low[p] = halves(field[p])
    forward_loop(meta, foot, high, low, rays)
    hand_out(rays, mine, theirs)


def second_kernel(meta, foot, *refs):
    pieces, (mine, theirs, field, sums, high, low, rays) = refs[:8], refs[8:]
    there_and_back(meta, foot, pieces, mine, theirs, field, high, low, rays)
    sums[0] = folded(field[...] * field[...])


def third_kernel(meta, foot, *refs):
    pieces, volume, grad = refs[:8], refs[8], refs[9]
    mine, theirs, field, sums, first, last, high, low, rays = refs[10:]
    there_and_back(meta, foot, pieces, mine, theirs, field, high, low, rays)
    sums[0] = folded(grad[...] * field[...])
    sums[1] = folded(field[...] * field[...])
    for p in range(field.shape[0]):
        cols = slice(128 * p, 128 * p + 128)
        first[0, p], last[0, p] = volume[0:8, cols], volume[24:32, cols]
        first[1, p], last[1, p] = grad[p, 0:8], grad[p, 24:32]
        first[2, p], last[2, p] = field[p, 0:8], field[p, 24:32]


def add_kernel(mine, got, kept, s1, s2, s3):
    for r, out in enumerate((kept, s1, s2, s3)):
        out[...] = mine[r] + got[r]


def tile_cols(ref):
    return jnp.stack([ref[:, 128 * t : 128 * t + 128] for t in range(ref.shape[1] // 128)])


def start_kernel(kept, a, b, c, measured, weights, residual, sent):
    value = kept[...] + a[...] + b[...] + c[...] - tile_cols(measured)
    residual[...] = value
    sent[...] = tile_cols(weights) * value


def middle_kernel(kept, a, b, c, weights, projected, sent, sums):
    value = kept[...] + a[...] + b[...] + c[...]
    weighted = tile_cols(weights) * value
    projected[...] = value
    sent[...] = weighted
    sums[0] = folded(weighted * value)


def as_rows(sums, rows):
    lane = lax.broadcasted_iota(jnp.int32, rows.shape, 1)
    value = jnp.zeros(rows.shape, F32)
    for n, part in enumerate(sums):
        value = jnp.where(lane == n, jnp.sum(part, keepdims=True), value)
    rows[...] = value


def end_kernel(kept, a, b, c, weights, before, norm0, curve0, turned, projected, rows):
    value = kept[...] + a[...] + b[...] + c[...]
    weighted = tile_cols(weights) * value
    projected[...] = value
    cross = folded(weighted * before[...])
    as_rows([norm0[0], curve0[0], turned[0], turned[1], cross, folded(weighted * value)], rows)


def totals(rows, count):
    value = jnp.sum(rows[...], axis=0, keepdims=True)
    return [jnp.sum(value[:, n : n + 1]) for n in range(count)]


def judge_kernel(rows, alphas, again):
    norm0, curve0, cross_g, square_g, cross_p, square_p = totals(rows, 6)
    alpha = norm0 / curve0
    norm1 = norm0 - 2.0 * alpha * cross_g + alpha * alpha * square_g
    curve1 = curve0 - 2.0 * alpha * cross_p + alpha * alpha * square_p
    sound = (norm1 > 0.01 * norm0) & (curve1 > 0.01 * curve0)
    for square in (square_g, square_p):
        sound = sound & (square > 1e-25) & (square < 1e37)
    alphas[0] = alpha
    alphas[1] = norm1 / curve1
    again[0] = jnp.where(sound, 0, 1)


def again_kernel(alphas, weights, p0, q0, grad, turned, rows):
    value = p0[...] - alphas[0] * q0[...]
    step = grad[...] - alphas[0] * turned[...]
    as_rows([folded(step * step), folded(tile_cols(weights) * value * value)], rows)


def ratio_kernel(alphas, rows, out):
    norm1, curve1 = totals(rows, 2)
    out[0] = alphas[0]
    out[1] = norm1 / curve1


def smooth_kernel(ends, alphas, volume, grad, turned, first, last, residual, p0, q0, smoothed, left_over):
    alpha0, alpha1 = alphas[0], alphas[1]
    rest = residual[...] - alpha0 * p0[...] - alpha1 * (p0[...] - alpha0 * q0[...])
    for t in range(rest.shape[0]):
        left_over[:, 128 * t : 128 * t + 128] = rest[t]

    def stepped(x, g, h):
        return x - alpha0 * g - alpha1 * (g - alpha0 * h)

    row = lax.broadcasted_iota(jnp.int32, (48, 128), 0)
    open_link = ~(((row == 7) & (ends[0] == 1)) | ((row == 39) & (ends[1] == 1)))
    link = jnp.where(open_link, F32(1.0), F32(0.0))
    for p in range(grad.shape[0]):
        cols = slice(128 * p, 128 * p + 128)
        ext = jnp.concatenate(
            [
                stepped(last[0, p], last[1, p], last[2, p]),
                stepped(volume[:, cols], grad[p], turned[p]),
                stepped(first[0, p], first[1, p], first[2, p]),
            ],
            axis=0,
        )
        for _ in range(PASSES):
            clipped = jnp.clip(pltpu.roll(ext, 47, 0) - ext, -huber_width, huber_width) * link
            ext = ext + smooth_rate * (clipped - pltpu.roll(clipped, 1, 0))
        smoothed[:, cols] = ext[8:40]


def shift(value, axis, by):
    n = lax.axis_size(axis)
    return lax.ppermute(value, axis, [(i, (i + by) % n) for i in range(n)])


RAY = (8, 32, 128)


def summed_by_owner(mine, theirs):
    got = shift(theirs, "tile_1", 1)
    kept, s1, s2, s3 = call(add_kernel, [RAY] * 4, [mine, got])
    moved = []
    for r, part in enumerate((s1, s2, s3), 1):
        moved.append(shift(part, "tile_0", r))
    return kept, *moved


def to_everyone(own):
    column = [own] + [shift(own, "tile_0", -r) for r in (1, 2, 3)]
    return column + [shift(block, "tile_1", 1) for block in column]


def from_all(rows):
    return lax.all_to_all(rows, TILE + SLAB, 0, 0, tiled=True)


def shards(volume, measured, weights, footprints, foot_pixel, foot_strip):
    owner = foot_strip // 32
    core = (owner & 1) ^ lax.axis_index("tile_1")
    ahead = ((owner >> 1) - lax.axis_index("tile_0")) & 3
    meta = (core * 4 + ahead) * 8 + (foot_strip // 4) % 8 + (foot_strip % 4) * 64 + foot_pixel * 256

    half, field = (4,) + RAY, (32, 32, 128)
    scratch = [pltpu.VMEM(field, BF16), pltpu.VMEM(field, BF16), pltpu.VMEM((64, 32, 128), F32)]
    mine, theirs = call(first_kernel, [half, half], [meta, footprints, volume], scratch, 1)
    parts = summed_by_owner(mine, theirs)
    residual, sent = call(start_kernel, [RAY, RAY], [*parts, measured, weights])

    mine, theirs, grad, norm0 = call(
        second_kernel, [half, half, field, (1, 8, 128)], [meta, footprints, *to_everyone(sent)], scratch, 1
    )
    parts = summed_by_owner(mine, theirs)
    p0, sent, curve0 = call(middle_kernel, [RAY, RAY, (1, 8, 128)], [*parts, weights])

    edge = (3, 32, 8, 128)
    mine, theirs, turned, sums, first, last = call(
        third_kernel,
        [half, half, field, (2, 8, 128), edge, edge],
        [meta, footprints, *to_everyone(sent), volume, grad],
        scratch,
        1,
    )
    slabs = lax.axis_size(SLAB)
    place_in = lax.axis_index(SLAB)
    ends = jnp.stack([place_in == 0, place_in == slabs - 1]).astype(jnp.int32)
    up = [(i, i + 1) for i in range(slabs - 1)]
    down = [(j, i) for i, j in up]
    last = lax.ppermute(last, SLAB, up)
    first = lax.ppermute(first, SLAB, down)
    parts = summed_by_owner(mine, theirs)
    everyone = slabs * lax.axis_size(TILE)
    q0, rows = call(
        end_kernel, [RAY, (everyone, 128)], [*parts, weights, p0, norm0, curve0, sums]
    )
    rows = from_all(rows)
    alphas, again = pl.pallas_call(
        judge_kernel,
        out_shape=[jax.ShapeDtypeStruct((2,), F32), jax.ShapeDtypeStruct((1,), jnp.int32)],
        in_specs=[VM],
        out_specs=[SM, SM],
        compiler_params=pltpu.CompilerParams(vmem_limit_bytes=8 << 20),
    )(rows)

    def summed_again(alphas):
        rows = call(
            again_kernel, [(everyone, 128)], [alphas, weights, p0, q0, grad, turned], (), 1
        )[0]
        return pl.pallas_call(
            ratio_kernel,
            out_shape=jax.ShapeDtypeStruct((2,), F32),
            in_specs=[SM, VM],
            out_specs=SM,
            compiler_params=pltpu.CompilerParams(vmem_limit_bytes=8 << 20),
        )(alphas, from_all(rows))

    alphas = lax.cond(again[0] == 1, summed_again, lambda known: known, alphas)
    return call(
        smooth_kernel,
        [volume.shape, measured.shape],
        [ends, alphas, volume, grad, turned, first, last, residual, p0, q0],
        (),
        2,
    )


def solution(mesh):
    finer = Mesh(mesh.devices.reshape(4, 2, 4, 4), ("tile_0", "tile_1", "slab_0", "slab_1"))
    return jax.shard_map(
        lambda *args: tuple(shards(*args)),
        mesh=finer,
        in_specs=(
            P(SLAB, TILE),
            P(SLAB, TILE),
            P(SLAB, TILE),
            P(TILE, None, None),
            P(TILE),
            P(TILE),
        ),
        out_specs=(P(SLAB, TILE), P(SLAB, TILE)),
        check_vma=False,
    )
```

profile of v0, /device:TPU:1, one launch (start us, length us, event | category | flops | bytes accessed | tf_op | source)
XLA Modules:
  0.0 115.4 jit_solution(8852172852516453073)
XLA Ops:
  1.4 2.2 %copy-done = f32[256,32,128]{2,1,0:T(8,128)S(1)} copy-done((f32[256,32,128]{2,1,0:T(8,128)S(1)}, f32[256,32,128]{2,1,0:T(8,128)}, u32[]{:S(2)}) %copy-start) | copy-done | bytes 4194328
  4.6 4.4 %shard_map.77 = (f32[4,8,32,128]{3,2,1,0:T(8,128)S(1)}, f32[4,8,32,128]{3,2,1,0:T(8,128)S(1)}) custom-call(s32[256]{0:T(256)S(1)} %multiply_add_fusion.meta, f32[256,32,128]{2,1,0:T(8,128)S(1)} %copy-done, f32[32,4096]{1,0:T(8,128)S(1)} %copy-done.2), custom_call_target="tpu_custom_call" | custom-call | flops 1000000 | bytes 1048576 | tf_op jit(solution)/shard_map/pallas_call | solution.py:26
  9.0 1.4 %collective-permute-start = (f32[4,8,32,128]{3,2,1,0:T(8,128)S(1)}, f32[4,8,32,128]{3,2,1,0:T(8,128)S(1)}, u32[]{:S(2)}, u32[]{:S(2)}) collective-permute-start(f32[4,8,32,128]{3,2,1,0:T(8,128)S(1)} %get-tuple-element.58), channel_id=1, source_target_pairs={{0,16},{16,0},{1,17},{17,1},{2,18},{18,2},{3,19},{19,3},{4,20},{20... | collective-permute-start | bytes 1572872 | tf_op jit(solution)/shard_map/ppermute | solution.py:241
  10.5 1.5 %collective-permute-done.got = f32[4,8,32,128]{3,2,1,0:T(8,128)S(1)} collective-permute-done((f32[4,8,32,128]{3,2,1,0:T(8,128)S(1)}, f32[4,8,32,128]{3,2,1,0:T(8,128)S(1)}, u32[]{:S(2)}, u32[]{:S(2)}) %collective-permute-start) | collective-permute-done | bytes 524320 | tf_op jit(solution)/shard_map/ppermute | solution.py:241
  12.1 1.5 %collective-permute-start.1 = (f32[8,32,128]{2,1,0:T(8,128)S(1)}, f32[8,32,128]{2,1,0:T(8,128)S(1)}, u32[]{:S(2)}, u32[]{:S(2)}) collective-permute-start(f32[8,32,128]{2,1,0:T(8,128)S(1)} %get-tuple-element.60), channel_id=1, source_target_pairs={{0,32},{32,64},{64,96},{96,0},{1,33},{33,65},{65,97},{97,1},{2,34}... | collective-permute-start | bytes 393224 | tf_op jit(solution)/shard_map/ppermute | solution.py:241
  13.6 2.6 %collective-permute-start.2 = (f32[8,32,128]{2,1,0:T(8,128)S(1)}, f32[8,32,128]{2,1,0:T(8,128)S(1)}, u32[]{:S(2)}, u32[]{:S(2)}) collective-permute-start(f32[8,32,128]{2,1,0:T(8,128)S(1)} %get-tuple-element.61), channel_id=1, source_target_pairs={{0,64},{32,96},{64,0},{96,32},{1,65},{33,97},{65,1},{97,33},{2,66}... | collective-permute-start | bytes 393224 | tf_op jit(solution)/shard_map/ppermute | solution.py:241
  17.3 1.2 %collective-permute-done.1.a = f32[8,32,128]{2,1,0:T(8,128)S(1)} collective-permute-done((f32[8,32,128]{2,1,0:T(8,128)S(1)}, f32[8,32,128]{2,1,0:T(8,128)S(1)}, u32[]{:S(2)}, u32[]{:S(2)}) %collective-permute-start.1) | collective-permute-done | bytes 131104 | tf_op jit(solution)/shard_map/ppermute | solution.py:241
  18.4 3.8 %collective-permute-done.2.b = f32[8,32,128]{2,1,0:T(8,128)S(1)} collective-permute-done((f32[8,32,128]{2,1,0:T(8,128)S(1)}, f32[8,32,128]{2,1,0:T(8,128)S(1)}, u32[]{:S(2)}, u32[]{:S(2)}) %collective-permute-start.2) | collective-permute-done | bytes 131104 | tf_op jit(solution)/shard_map/ppermute | solution.py:241
  23.3 2.3 %collective-permute-start.5 = (f32[8,32,128]{2,1,0:T(8,128)S(1)}, f32[8,32,128]{2,1,0:T(8,128)S(1)}, u32[]{:S(2)}, u32[]{:S(2)}) collective-permute-start(f32[8,32,128]{2,1,0:T(8,128)S(1)} %get-tuple-element.63.refs_0_), channel_id=1, source_target_pairs={{0,64},{32,96},{64,0},{96,32},{1,65},{33,97},{65,1},{97,33},{2,66}... | collective-permute-start | bytes 393224 | tf_op jit(solution)/shard_map/ppermute | solution.py:241
  26.5 2.3 %collective-permute-start.7 = (f32[8,32,128]{2,1,0:T(8,128)S(1)}, f32[8,32,128]{2,1,0:T(8,128)S(1)}, u32[]{:S(2)}, u32[]{:S(2)}) collective-permute-start(f32[8,32,128]{2,1,0:T(8,128)S(1)} %get-tuple-element.63.refs_0_), channel_id=1, source_target_pairs={{0,16},{16,0},{1,17},{17,1},{2,18},{18,2},{3,19},{19,3},{4,20},{20... | collective-permute-start | bytes 393224 | tf_op jit(solution)/shard_map/ppermute | solution.py:241
  28.8 2.2 %collective-permute-start.10 = (f32[8,32,128]{2,1,0:T(8,128)S(1)}, f32[8,32,128]{2,1,0:T(8,128)S(1)}, u32[]{:S(2)}, u32[]{:S(2)}) collective-permute-start(f32[8,32,128]{2,1,0:T(8,128)S(1)} %collective-permute-done.6.refs_3_), channel_id=1, source_target_pairs={{0,16},{16,0},{1,17},{17,1},{2,18},{18,2},{3,19},{19,3},{4,20},{20... | collective-permute-start | bytes 393224 | tf_op jit(solution)/shard_map/ppermute | solution.py:241
  31.0 1.9 %collective-permute-start.9 = (f32[8,32,128]{2,1,0:T(8,128)S(1)}, f32[8,32,128]{2,1,0:T(8,128)S(1)}, u32[]{:S(2)}, u32[]{:S(2)}) collective-permute-start(f32[8,32,128]{2,1,0:T(8,128)S(1)} %collective-permute-done.5.refs_2_), channel_id=1, source_target_pairs={{0,16},{16,0},{1,17},{17,1},{2,18},{18,2},{3,19},{19,3},{4,20},{20... | collective-permute-start | bytes 393224 | tf_op jit(solution)/shard_map/ppermute | solution.py:241
  34.2 7.0 %shard_map.80 = (f32[4,8,32,128]{3,2,1,0:T(8,128)S(1)}, f32[4,8,32,128]{3,2,1,0:T(8,128)S(1)}, f32[32,32,128]{2,1,0:T(8,128)S(1)}, f32[1,8,128]{2,1,0:T(8,128)S(1)}) custom-call(s32[256]{0:T(256)S(1)} %multiply_add_fusion.meta, f32[256,32,128]{2,1,0:T(8,128)S(1)} %copy-done.1, f32[8,32,128]{2,1,0:T(8,128)S(1)} %get-tuple-element.63.refs_0_, ...), custom_call_target="tpu_custom_call" | custom-call | flops 1000000 | bytes 1048576 | tf_op jit(solution)/shard_map/pallas_call | solution.py:26
  41.5 1.7 %collective-permute-done.11.got = f32[4,8,32,128]{3,2,1,0:T(8,128)S(1)} collective-permute-done((f32[4,8,32,128]{3,2,1,0:T(8,128)S(1)}, f32[4,8,32,128]{3,2,1,0:T(8,128)S(1)}, u32[]{:S(2)}, u32[]{:S(2)}) %collective-permute-start.11) | collective-permute-done | bytes 524320 | tf_op jit(solution)/shard_map/ppermute | solution.py:241
  44.4 2.1 %collective-permute-start.13 = (f32[8,32,128]{2,1,0:T(8,128)S(1)}, f32[8,32,128]{2,1,0:T(8,128)S(1)}, u32[]{:S(2)}, u32[]{:S(2)}) collective-permute-start(f32[8,32,128]{2,1,0:T(8,128)S(1)} %get-tuple-element.68), channel_id=1, source_target_pairs={{0,64},{32,96},{64,0},{96,32},{1,65},{33,97},{65,1},{97,33},{2,66}... | collective-permute-start | bytes 393224 | tf_op jit(solution)/shard_map/ppermute | solution.py:241
  47.1 2.3 %collective-permute-done.12.a = f32[8,32,128]{2,1,0:T(8,128)S(1)} collective-permute-done((f32[8,32,128]{2,1,0:T(8,128)S(1)}, f32[8,32,128]{2,1,0:T(8,128)S(1)}, u32[]{:S(2)}, u32[]{:S(2)}) %collective-permute-start.12) | collective-permute-done | bytes 131104 | tf_op jit(solution)/shard_map/ppermute | solution.py:241
  49.4 3.1 %collective-permute-done.13.b = f32[8,32,128]{2,1,0:T(8,128)S(1)} collective-permute-done((f32[8,32,128]{2,1,0:T(8,128)S(1)}, f32[8,32,128]{2,1,0:T(8,128)S(1)}, u32[]{:S(2)}, u32[]{:S(2)}) %collective-permute-start.13) | collective-permute-done | bytes 131104 | tf_op jit(solution)/shard_map/ppermute | solution.py:241
  52.7 1.9 %collective-permute-start.17 = (f32[8,32,128]{2,1,0:T(8,128)S(1)}, f32[8,32,128]{2,1,0:T(8,128)S(1)}, u32[]{:S(2)}, u32[]{:S(2)}) collective-permute-start(f32[8,32,128]{2,1,0:T(8,128)S(1)} %get-tuple-element.70.refs_0_), channel_id=1, source_target_pairs={{0,32},{32,64},{64,96},{96,0},{1,33},{33,65},{65,97},{97,1},{2,34}... | collective-permute-start | bytes 393224 | tf_op jit(solution)/shard_map/ppermute | solution.py:241
  54.6 2.5 %collective-permute-start.16 = (f32[8,32,128]{2,1,0:T(8,128)S(1)}, f32[8,32,128]{2,1,0:T(8,128)S(1)}, u32[]{:S(2)}, u32[]{:S(2)}) collective-permute-start(f32[8,32,128]{2,1,0:T(8,128)S(1)} %get-tuple-element.70.refs_0_), channel_id=1, source_target_pairs={{0,64},{32,96},{64,0},{96,32},{1,65},{33,97},{65,1},{97,33},{2,66}... | collective-permute-start | bytes 393224 | tf_op jit(solution)/shard_map/ppermute | solution.py:241
  57.1 1.5 %collective-permute-start.18 = (f32[8,32,128]{2,1,0:T(8,128)S(1)}, f32[8,32,128]{2,1,0:T(8,128)S(1)}, u32[]{:S(2)}, u32[]{:S(2)}) collective-permute-start(f32[8,32,128]{2,1,0:T(8,128)S(1)} %get-tuple-element.70.refs_0_), channel_id=1, source_target_pairs={{0,16},{16,0},{1,17},{17,1},{2,18},{18,2},{3,19},{19,3},{4,20},{20... | collective-permute-start | bytes 393224 | tf_op jit(solution)/shard_map/ppermute | solution.py:241
  58.6 1.7 %collective-permute-start.21 = (f32[8,32,128]{2,1,0:T(8,128)S(1)}, f32[8,32,128]{2,1,0:T(8,128)S(1)}, u32[]{:S(2)}, u32[]{:S(2)}) collective-permute-start(f32[8,32,128]{2,1,0:T(8,128)S(1)} %collective-permute-done.17.refs_3_), channel_id=1, source_target_pairs={{0,16},{16,0},{1,17},{17,1},{2,18},{18,2},{3,19},{19,3},{4,20},{20... | collective-permute-start | bytes 393224 | tf_op jit(solution)/shard_map/ppermute | solution.py:241
  60.3 2.6 %collective-permute-done.16.refs_2_ = f32[8,32,128]{2,1,0:T(8,128)S(1)} collective-permute-done((f32[8,32,128]{2,1,0:T(8,128)S(1)}, f32[8,32,128]{2,1,0:T(8,128)S(1)}, u32[]{:S(2)}, u32[]{:S(2)}) %collective-permute-start.16) | collective-permute-done | bytes 131104 | tf_op jit(solution)/shard_map/ppermute | solution.py:241
  62.9 1.4 %collective-permute-start.20 = (f32[8,32,128]{2,1,0:T(8,128)S(1)}, f32[8,32,128]{2,1,0:T(8,128)S(1)}, u32[]{:S(2)}, u32[]{:S(2)}) collective-permute-start(f32[8,32,128]{2,1,0:T(8,128)S(1)} %collective-permute-done.16.refs_2_), channel_id=1, source_target_pairs={{0,16},{16,0},{1,17},{17,1},{2,18},{18,2},{3,19},{19,3},{4,20},{20... | collective-permute-start | bytes 393224 | tf_op jit(solution)/shard_map/ppermute | solution.py:241
  65.7 7.5 %shard_map.83 = (f32[4,8,32,128]{3,2,1,0:T(8,128)S(1)}, f32[4,8,32,128]{3,2,1,0:T(8,128)S(1)}, f32[32,32,128]{2,1,0:T(8,128)}, f32[2,8,128]{2,1,0:T(8,128)S(1)},...) custom-call(s32[256]{0:T(256)S(1)} %multiply_add_fusion.meta, f32[256,32,128]{2,1,0:T(8,128)S(1)} %copy-done.1, ...), custom_call_target="tpu_custom_call" | custom-call | flops 1000000 | bytes 1048576 | tf_op jit(solution)/shard_map/pallas_call | solution.py:26
  73.4 1.3 %collective-permute-start.26 = (f32[3,32,8,128]{3,2,1,0:T(8,128)S(1)}, f32[3,32,8,128]{3,2,1,0:T(8,128)S(1)}, u32[]{:S(2)}, u32[]{:S(2)}) collective-permute-start(f32[3,32,8,128]{3,2,1,0:T(8,128)S(1)} %get-tuple-element.87), channel_id=1, source_target_pairs={{1,0},{2,1},{3,2},{4,3},{5,4},{6,5},{7,6},{8,7},{9,8},{10,9},{11,1... | collective-permute-start | bytes 1179656 | tf_op jit(solution)/shard_map/ppermute | solution.py:297
  74.7 4.0 %collective-permute-start.27 = (f32[3,32,8,128]{3,2,1,0:T(8,128)S(1)}, f32[3,32,8,128]{3,2,1,0:T(8,128)S(1)}, u32[]{:S(2)}, u32[]{:S(2)}) collective-permute-start(f32[3,32,8,128]{3,2,1,0:T(8,128)S(1)} %get-tuple-element.88), channel_id=1, source_target_pairs={{0,1},{1,2},{2,3},{3,4},{4,5},{5,6},{6,7},{7,8},{8,9},{9,10},{10,1... | collective-permute-start | bytes 1179656 | tf_op jit(solution)/shard_map/ppermute | solution.py:296
  79.2 2.5 %collective-permute-start.24 = (f32[8,32,128]{2,1,0:T(8,128)S(1)}, f32[8,32,128]{2,1,0:T(8,128)S(1)}, u32[]{:S(2)}, u32[]{:S(2)}) collective-permute-start(f32[8,32,128]{2,1,0:T(8,128)S(1)} %get-tuple-element.76), channel_id=1, source_target_pairs={{0,64},{32,96},{64,0},{96,32},{1,65},{33,97},{65,1},{97,33},{2,66}... | collective-permute-start | bytes 393224 | tf_op jit(solution)/shard_map/ppermute | solution.py:241
  81.9 2.3 %collective-permute-done.23.a = f32[8,32,128]{2,1,0:T(8,128)S(1)} collective-permute-done((f32[8,32,128]{2,1,0:T(8,128)S(1)}, f32[8,32,128]{2,1,0:T(8,128)S(1)}, u32[]{:S(2)}, u32[]{:S(2)}) %collective-permute-start.23) | collective-permute-done | bytes 131104 | tf_op jit(solution)/shard_map/ppermute | solution.py:241
  84.2 3.2 %collective-permute-done.24.b = f32[8,32,128]{2,1,0:T(8,128)S(1)} collective-permute-done((f32[8,32,128]{2,1,0:T(8,128)S(1)}, f32[8,32,128]{2,1,0:T(8,128)S(1)}, u32[]{:S(2)}, u32[]{:S(2)}) %collective-permute-start.24) | collective-permute-done | bytes 131104 | tf_op jit(solution)/shard_map/ppermute | solution.py:241
  88.3 13.0 %all-to-all-start.1 = ((f32[128,1,128]{2,1,0:T(1,128)}), f32[128,1,128]{2,1,0:T(1,128)S(1)}, u32[]{:S(2)}, u32[]{:S(2)}) async-start(f32[128,1,128]{2,1,0:T(1,128)} %bitcast.7), calls=%async_computation.1 | async-start | bytes 131072 | tf_op jit(solution)/shard_map/all_to_all | solution.py:262
  101.4 9.7 %all-to-all-done.1 = f32[128,1,128]{2,1,0:T(1,128)S(1)} async-done(((f32[128,1,128]{2,1,0:T(1,128)}), f32[128,1,128]{2,1,0:T(1,128)S(1)}, u32[]{:S(2)}, u32[]{:S(2)}) %all-to-all-start.1) | async-done | bytes 65568 | tf_op jit(solution)/shard_map/all_to_all | solution.py:262
  112.5 2.9 %shard_map.87 = (f32[32,4096]{1,0:T(8,128)}, f32[32,1024]{1,0:T(8,128)}) custom-call(s32[2]{0:T(128)S(1)} %add_convert_fusion.ends, f32[2]{0:T(128)S(1)} %get-tuple-element.90.alphas, f32[32,4096]{1,0:T(8,128)S(1)} %copy-done.3, f32[32,32,128]{2,1,0:T(8,128)} %copy-done.5, f32[32,32,128]{2,1,0:T(8,128)} %get-tuple-element.86.turned, ...), custom_call_target="tpu_custom_call" | custom-call | flops 1000000 | bytes 1048576 | tf_op jit(solution)/shard_map/pallas_call | solution.py:26
  (54 shorter events, 12.4 us)
Async XLA Ops:
  4.6 29.6 %copy-start.1 = (f32[256,32,128]{2,1,0:T(8,128)S(1)}, f32[256,32,128]{2,1,0:T(8,128)}, u32[]{:S(2)}) copy-start(f32[256,32,128]{2,1,0:T(8,128)} %foot.5) | copy-start | bytes 12582916
  9.0 3.0 %collective-permute-start = (f32[4,8,32,128]{3,2,1,0:T(8,128)S(1)}, f32[4,8,32,128]{3,2,1,0:T(8,128)S(1)}, u32[]{:S(2)}, u32[]{:S(2)}) collective-permute-start(f32[4,8,32,128]{3,2,1,0:T(8,128)S(1)} %get-tuple-element.58), channel_id=1, source_target_pairs={{0,16},{16,0},{1,17},{17,1},{2,18},{18,2},{3,19},{19,3},{4,20},{20... | collective-permute-start | bytes 1572872 | tf_op jit(solution)/shard_map/ppermute | solution.py:241
  12.0 53.6 %copy-start.3 = (f32[32,4096]{1,0:T(8,128)S(1)}, f32[32,4096]{1,0:T(8,128)}, u32[]{:S(2)}) copy-start(f32[32,4096]{1,0:T(8,128)} %volume.3) | copy-start | bytes 1572868
  12.1 6.3 %collective-permute-start.1 = (f32[8,32,128]{2,1,0:T(8,128)S(1)}, f32[8,32,128]{2,1,0:T(8,128)S(1)}, u32[]{:S(2)}, u32[]{:S(2)}) collective-permute-start(f32[8,32,128]{2,1,0:T(8,128)S(1)} %get-tuple-element.60), channel_id=1, source_target_pairs={{0,32},{32,64},{64,96},{96,0},{1,33},{33,65},{65,97},{97,1},{2,34}... | collective-permute-start | bytes 393224 | tf_op jit(solution)/shard_map/ppermute | solution.py:241
  13.6 8.7 %collective-permute-start.2 = (f32[8,32,128]{2,1,0:T(8,128)S(1)}, f32[8,32,128]{2,1,0:T(8,128)S(1)}, u32[]{:S(2)}, u32[]{:S(2)}) collective-permute-start(f32[8,32,128]{2,1,0:T(8,128)S(1)} %get-tuple-element.61), channel_id=1, source_target_pairs={{0,64},{32,96},{64,0},{96,32},{1,65},{33,97},{65,1},{97,33},{2,66}... | collective-permute-start | bytes 393224 | tf_op jit(solution)/shard_map/ppermute | solution.py:241
  16.2 6.0 %collective-permute-start.3 = (f32[8,32,128]{2,1,0:T(8,128)S(1)}, f32[8,32,128]{2,1,0:T(8,128)S(1)}, u32[]{:S(2)}, u32[]{:S(2)}) collective-permute-start(f32[8,32,128]{2,1,0:T(8,128)S(1)} %get-tuple-element.62), channel_id=1, source_target_pairs={{0,96},{32,0},{64,32},{96,64},{1,97},{33,1},{65,33},{97,65},{2,98}... | collective-permute-start | bytes 393224 | tf_op jit(solution)/shard_map/ppermute | solution.py:241
  22.3 6.5 %collective-permute-start.6 = (f32[8,32,128]{2,1,0:T(8,128)S(1)}, f32[8,32,128]{2,1,0:T(8,128)S(1)}, u32[]{:S(2)}, u32[]{:S(2)}) collective-permute-start(f32[8,32,128]{2,1,0:T(8,128)S(1)} %get-tuple-element.63.refs_0_), channel_id=1, source_target_pairs={{0,32},{32,64},{64,96},{96,0},{1,33},{33,65},{65,97},{97,1},{2,34}... | collective-permute-start | bytes 393224 | tf_op jit(solution)/shard_map/ppermute | solution.py:241
  23.3 7.6 %collective-permute-start.5 = (f32[8,32,128]{2,1,0:T(8,128)S(1)}, f32[8,32,128]{2,1,0:T(8,128)S(1)}, u32[]{:S(2)}, u32[]{:S(2)}) collective-permute-start(f32[8,32,128]{2,1,0:T(8,128)S(1)} %get-tuple-element.63.refs_0_), channel_id=1, source_target_pairs={{0,64},{32,96},{64,0},{96,32},{1,65},{33,97},{65,1},{97,33},{2,66}... | collective-permute-start | bytes 393224 | tf_op jit(solution)/shard_map/ppermute | solution.py:241
  25.6 7.3 %collective-permute-start.4 = (f32[8,32,128]{2,1,0:T(8,128)S(1)}, f32[8,32,128]{2,1,0:T(8,128)S(1)}, u32[]{:S(2)}, u32[]{:S(2)}) collective-permute-start(f32[8,32,128]{2,1,0:T(8,128)S(1)} %get-tuple-element.63.refs_0_), channel_id=1, source_target_pairs={{0,96},{32,0},{64,32},{96,64},{1,97},{33,1},{65,33},{97,65},{2,98}... | collective-permute-start | bytes 393224 | tf_op jit(solution)/shard_map/ppermute | solution.py:241
  26.5 6.4 %collective-permute-start.7 = (f32[8,32,128]{2,1,0:T(8,128)S(1)}, f32[8,32,128]{2,1,0:T(8,128)S(1)}, u32[]{:S(2)}, u32[]{:S(2)}) collective-permute-start(f32[8,32,128]{2,1,0:T(8,128)S(1)} %get-tuple-element.63.refs_0_), channel_id=1, source_target_pairs={{0,16},{16,0},{1,17},{17,1},{2,18},{18,2},{3,19},{19,3},{4,20},{20... | collective-permute-start | bytes 393224 | tf_op jit(solution)/shard_map/ppermute | solution.py:241
  28.8 4.1 %collective-permute-start.10 = (f32[8,32,128]{2,1,0:T(8,128)S(1)}, f32[8,32,128]{2,1,0:T(8,128)S(1)}, u32[]{:S(2)}, u32[]{:S(2)}) collective-permute-start(f32[8,32,128]{2,1,0:T(8,128)S(1)} %collective-permute-done.6.refs_3_), channel_id=1, source_target_pairs={{0,16},{16,0},{1,17},{17,1},{2,18},{18,2},{3,19},{19,3},{4,20},{20... | collective-permute-start | bytes 393224 | tf_op jit(solution)/shard_map/ppermute | solution.py:241
  31.0 2.9 %collective-permute-start.9 = (f32[8,32,128]{2,1,0:T(8,128)S(1)}, f32[8,32,128]{2,1,0:T(8,128)S(1)}, u32[]{:S(2)}, u32[]{:S(2)}) collective-permute-start(f32[8,32,128]{2,1,0:T(8,128)S(1)} %collective-permute-done.5.refs_2_), channel_id=1, source_target_pairs={{0,16},{16,0},{1,17},{17,1},{2,18},{18,2},{3,19},{19,3},{4,20},{20... | collective-permute-start | bytes 393224 | tf_op jit(solution)/shard_map/ppermute | solution.py:241
  32.9 1.3 %collective-permute-start.8 = (f32[8,32,128]{2,1,0:T(8,128)S(1)}, f32[8,32,128]{2,1,0:T(8,128)S(1)}, u32[]{:S(2)}, u32[]{:S(2)}) collective-permute-start(f32[8,32,128]{2,1,0:T(8,128)S(1)} %collective-permute-done.4.refs_1_), channel_id=1, source_target_pairs={{0,16},{16,0},{1,17},{17,1},{2,18},{18,2},{3,19},{19,3},{4,20},{20... | collective-permute-start | bytes 393224 | tf_op jit(solution)/shard_map/ppermute | solution.py:241
  41.2 37.5 %copy-start.5 = (f32[32,32,128]{2,1,0:T(8,128)}, f32[32,32,128]{2,1,0:T(8,128)S(1)}, u32[]{:S(2)}) copy-start(f32[32,32,128]{2,1,0:T(8,128)S(1)} %get-tuple-element.71.refs_9_.grad) | copy-start | bytes 1572868
  41.3 2.0 %collective-permute-start.11 = (f32[4,8,32,128]{3,2,1,0:T(8,128)S(1)}, f32[4,8,32,128]{3,2,1,0:T(8,128)S(1)}, u32[]{:S(2)}, u32[]{:S(2)}) collective-permute-start(f32[4,8,32,128]{3,2,1,0:T(8,128)S(1)} %get-tuple-element.65), channel_id=1, source_target_pairs={{0,16},{16,0},{1,17},{17,1},{2,18},{18,2},{3,19},{19,3},{4,20},{20... | collective-permute-start | bytes 1572872 | tf_op jit(solution)/shard_map/ppermute | solution.py:241
  43.3 6.1 %collective-permute-start.12 = (f32[8,32,128]{2,1,0:T(8,128)S(1)}, f32[8,32,128]{2,1,0:T(8,128)S(1)}, u32[]{:S(2)}, u32[]{:S(2)}) collective-permute-start(f32[8,32,128]{2,1,0:T(8,128)S(1)} %get-tuple-element.67), channel_id=1, source_target_pairs={{0,32},{32,64},{64,96},{96,0},{1,33},{33,65},{65,97},{97,1},{2,34}... | collective-permute-start | bytes 393224 | tf_op jit(solution)/shard_map/ppermute | solution.py:241
  44.4 8.2 %collective-permute-start.13 = (f32[8,32,128]{2,1,0:T(8,128)S(1)}, f32[8,32,128]{2,1,0:T(8,128)S(1)}, u32[]{:S(2)}, u32[]{:S(2)}) collective-permute-start(f32[8,32,128]{2,1,0:T(8,128)S(1)} %get-tuple-element.68), channel_id=1, source_target_pairs={{0,64},{32,96},{64,0},{96,32},{1,65},{33,97},{65,1},{97,33},{2,66}... | collective-permute-start | bytes 393224 | tf_op jit(solution)/shard_map/ppermute | solution.py:241
  46.6 6.0 %collective-permute-start.14 = (f32[8,32,128]{2,1,0:T(8,128)S(1)}, f32[8,32,128]{2,1,0:T(8,128)S(1)}, u32[]{:S(2)}, u32[]{:S(2)}) collective-permute-start(f32[8,32,128]{2,1,0:T(8,128)S(1)} %get-tuple-element.69), channel_id=1, source_target_pairs={{0,96},{32,0},{64,32},{96,64},{1,97},{33,1},{65,33},{97,65},{2,98}... | collective-permute-start | bytes 393224 | tf_op jit(solution)/shard_map/ppermute | solution.py:241
  52.7 6.0 %collective-permute-start.17 = (f32[8,32,128]{2,1,0:T(8,128)S(1)}, f32[8,32,128]{2,1,0:T(8,128)S(1)}, u32[]{:S(2)}, u32[]{:S(2)}) collective-permute-start(f32[8,32,128]{2,1,0:T(8,128)S(1)} %get-tuple-element.70.refs_0_), channel_id=1, source_target_pairs={{0,32},{32,64},{64,96},{96,0},{1,33},{33,65},{65,97},{97,1},{2,34}... | collective-permute-start | bytes 393224 | tf_op jit(solution)/shard_map/ppermute | solution.py:241
  54.6 8.3 %collective-permute-start.16 = (f32[8,32,128]{2,1,0:T(8,128)S(1)}, f32[8,32,128]{2,1,0:T(8,128)S(1)}, u32[]{:S(2)}, u32[]{:S(2)}) collective-permute-start(f32[8,32,128]{2,1,0:T(8,128)S(1)} %get-tuple-element.70.refs_0_), channel_id=1, source_target_pairs={{0,64},{32,96},{64,0},{96,32},{1,65},{33,97},{65,1},{97,33},{2,66}... | collective-permute-start | bytes 393224 | tf_op jit(solution)/shard_map/ppermute | solution.py:241
  57.0 7.3 %collective-permute-start.15 = (f32[8,32,128]{2,1,0:T(8,128)S(1)}, f32[8,32,128]{2,1,0:T(8,128)S(1)}, u32[]{:S(2)}, u32[]{:S(2)}) collective-permute-start(f32[8,32,128]{2,1,0:T(8,128)S(1)} %get-tuple-element.70.refs_0_), channel_id=1, source_target_pairs={{0,96},{32,0},{64,32},{96,64},{1,97},{33,1},{65,33},{97,65},{2,98}... | collective-permute-start | bytes 393224 | tf_op jit(solution)/shard_map/ppermute | solution.py:241
  57.1 7.2 %collective-permute-start.18 = (f32[8,32,128]{2,1,0:T(8,128)S(1)}, f32[8,32,128]{2,1,0:T(8,128)S(1)}, u32[]{:S(2)}, u32[]{:S(2)}) collective-permute-start(f32[8,32,128]{2,1,0:T(8,128)S(1)} %get-tuple-element.70.refs_0_), channel_id=1, source_target_pairs={{0,16},{16,0},{1,17},{17,1},{2,18},{18,2},{3,19},{19,3},{4,20},{20... | collective-permute-start | bytes 393224 | tf_op jit(solution)/shard_map/ppermute | solution.py:241
  58.6 5.7 %collective-permute-start.21 = (f32[8,32,128]{2,1,0:T(8,128)S(1)}, f32[8,32,128]{2,1,0:T(8,128)S(1)}, u32[]{:S(2)}, u32[]{:S(2)}) collective-permute-start(f32[8,32,128]{2,1,0:T(8,128)S(1)} %collective-permute-done.17.refs_3_), channel_id=1, source_target_pairs={{0,16},{16,0},{1,17},{17,1},{2,18},{18,2},{3,19},{19,3},{4,20},{20... | collective-permute-start | bytes 393224 | tf_op jit(solution)/shard_map/ppermute | solution.py:241
  62.9 2.4 %collective-permute-start.20 = (f32[8,32,128]{2,1,0:T(8,128)S(1)}, f32[8,32,128]{2,1,0:T(8,128)S(1)}, u32[]{:S(2)}, u32[]{:S(2)}) collective-permute-start(f32[8,32,128]{2,1,0:T(8,128)S(1)} %collective-permute-done.16.refs_2_), channel_id=1, source_target_pairs={{0,16},{16,0},{1,17},{17,1},{2,18},{18,2},{3,19},{19,3},{4,20},{20... | collective-permute-start | bytes 393224 | tf_op jit(solution)/shard_map/ppermute | solution.py:241
  64.3 1.3 %collective-permute-start.19 = (f32[8,32,128]{2,1,0:T(8,128)S(1)}, f32[8,32,128]{2,1,0:T(8,128)S(1)}, u32[]{:S(2)}, u32[]{:S(2)}) collective-permute-start(f32[8,32,128]{2,1,0:T(8,128)S(1)} %collective-permute-done.15.refs_1_), channel_id=1, source_target_pairs={{0,16},{16,0},{1,17},{17,1},{2,18},{18,2},{3,19},{19,3},{4,20},{20... | collective-permute-start | bytes 393224 | tf_op jit(solution)/shard_map/ppermute | solution.py:241
  73.2 5.5 %collective-permute-start.22 = (f32[4,8,32,128]{3,2,1,0:T(8,128)S(1)}, f32[4,8,32,128]{3,2,1,0:T(8,128)S(1)}, u32[]{:S(2)}, u32[]{:S(2)}) collective-permute-start(f32[4,8,32,128]{3,2,1,0:T(8,128)S(1)} %get-tuple-element.73), channel_id=1, source_target_pairs={{0,16},{16,0},{1,17},{17,1},{2,18},{18,2},{3,19},{19,3},{4,20},{20... | collective-permute-start | bytes 1572872 | tf_op jit(solution)/shard_map/ppermute | solution.py:241
  73.4 39.1 %collective-permute-start.26 = (f32[3,32,8,128]{3,2,1,0:T(8,128)S(1)}, f32[3,32,8,128]{3,2,1,0:T(8,128)S(1)}, u32[]{:S(2)}, u32[]{:S(2)}) collective-permute-start(f32[3,32,8,128]{3,2,1,0:T(8,128)S(1)} %get-tuple-element.87), channel_id=1, source_target_pairs={{1,0},{2,1},{3,2},{4,3},{5,4},{6,5},{7,6},{8,7},{9,8},{10,9},{11,1... | collective-permute-start | bytes 1179656 | tf_op jit(solution)/shard_map/ppermute | solution.py:297
  74.7 37.9 %collective-permute-start.27 = (f32[3,32,8,128]{3,2,1,0:T(8,128)S(1)}, f32[3,32,8,128]{3,2,1,0:T(8,128)S(1)}, u32[]{:S(2)}, u32[]{:S(2)}) collective-permute-start(f32[3,32,8,128]{3,2,1,0:T(8,128)S(1)} %get-tuple-element.88), channel_id=1, source_target_pairs={{0,1},{1,2},{2,3},{3,4},{4,5},{5,6},{6,7},{7,8},{8,9},{9,10},{10,1... | collective-permute-start | bytes 1179656 | tf_op jit(solution)/shard_map/ppermute | solution.py:296
  78.8 5.5 %collective-permute-start.23 = (f32[8,32,128]{2,1,0:T(8,128)S(1)}, f32[8,32,128]{2,1,0:T(8,128)S(1)}, u32[]{:S(2)}, u32[]{:S(2)}) collective-permute-start(f32[8,32,128]{2,1,0:T(8,128)S(1)} %get-tuple-element.75), channel_id=1, source_target_pairs={{0,32},{32,64},{64,96},{96,0},{1,33},{33,65},{65,97},{97,1},{2,34}... | collective-permute-start | bytes 393224 | tf_op jit(solution)/shard_map/ppermute | solution.py:241
  79.2 8.2 %collective-permute-start.24 = (f32[8,32,128]{2,1,0:T(8,128)S(1)}, f32[8,32,128]{2,1,0:T(8,128)S(1)}, u32[]{:S(2)}, u32[]{:S(2)}) collective-permute-start(f32[8,32,128]{2,1,0:T(8,128)S(1)} %get-tuple-element.76), channel_id=1, source_target_pairs={{0,64},{32,96},{64,0},{96,32},{1,65},{33,97},{65,1},{97,33},{2,66}... | collective-permute-start | bytes 393224 | tf_op jit(solution)/shard_map/ppermute | solution.py:241
  81.7 5.8 %collective-permute-start.25 = (f32[8,32,128]{2,1,0:T(8,128)S(1)}, f32[8,32,128]{2,1,0:T(8,128)S(1)}, u32[]{:S(2)}, u32[]{:S(2)}) collective-permute-start(f32[8,32,128]{2,1,0:T(8,128)S(1)} %get-tuple-element.77), channel_id=1, source_target_pairs={{0,96},{32,0},{64,32},{96,64},{1,97},{33,1},{65,33},{97,65},{2,98}... | collective-permute-start | bytes 393224 | tf_op jit(solution)/shard_map/ppermute | solution.py:241
  88.3 22.7 %all-to-all-start.1 = ((f32[128,1,128]{2,1,0:T(1,128)}), f32[128,1,128]{2,1,0:T(1,128)S(1)}, u32[]{:S(2)}, u32[]{:S(2)}) async-start(f32[128,1,128]{2,1,0:T(1,128)} %bitcast.7), calls=%async_computation.1 | async-start | bytes 131072 | tf_op jit(solution)/shard_map/all_to_all | solution.py:262
  (4 other events, 38.5 us)
where the time goes:
time: 116 us; the launch traced here: 115 us
  starting transfers between devices  52 us (45%)
  waiting for transfers between devices  34.2 us (29%)
  Pallas kernels  23.8 us (21%)
  local copies, waits for them, and re-layouts  3.24 us (3%)
  between operations  1.45 us (1%)
    ppermute x26, starting transfers between devices, shift(): return lax.ppermute(value, axis, [(i, (i + by) % n) for i in range(n)])  33.7 us
    ppermute x26, waiting for transfers between devices, shift(): return lax.ppermute(value, axis, [(i, (i + by) % n) for i in range(n)])  24.5 us
    pallas_call x10, Pallas kernels, call(): pl.pallas_call(kernel, out_shape=[jax.ShapeDtypeStruct(s, F32) for s in o...  23 us
    all_to_all x1, starting transfers between devices, from_all(): return lax.all_to_all(rows, TILE + SLAB, 0, 0, tiled=True)  13 us
    all_to_all x1, waiting for transfers between devices, from_all(): return lax.all_to_all(rows, TILE + SLAB, 0, 0, tiled=True)  9.66 us
    ppermute x1, starting transfers between devices, shards(): last = lax.ppermute(last, SLAB, up)  4.01 us
    unnamed x14, local copies, waits for them, and re-layouts  3.24 us
  transfers between devices with their start and end apart: 29, of which 15 were waited for; matrix products, arithmetic and copies ran while one was open for 0% of the time, Pallas kernels for 1%

commit v1 on v0

v1 whole, which is shorter than its diff:
```python
import jax
import jax.numpy as jnp
from jax import lax
from jax.experimental import pallas as pl
from jax.experimental.pallas import tpu as pltpu
from jax.sharding import Mesh
from jax.sharding import PartitionSpec as P

PASSES = 3
TILE = ("tile_0", "tile_1")
SLAB = ("slab_0", "slab_1")
GROUP = 4
UNROLL = 16
CHUNKS = 4

huber_width = 0.5
smooth_rate = 0.2


VM = pl.BlockSpec(memory_space=pltpu.VMEM)
SM = pl.BlockSpec(memory_space=pltpu.SMEM)
AN = pl.BlockSpec(memory_space=pltpu.HBM)
F32 = jnp.float32
BF16 = jnp.bfloat16


def call(kernel, outs, ins, scratch=(), smem=0, flops=1000000, limit=24, any_at=()):
    specs = [AN if n in any_at else SM if n < smem else VM for n in range(len(ins))]
    return pl.pallas_call(
        kernel,
        out_shape=[s if hasattr(s, "dtype") else jax.ShapeDtypeStruct(s, F32) for s in outs],
        in_specs=specs,
        out_specs=[VM] * len(outs),
        scratch_shapes=list(scratch),
        compiler_params=pltpu.CompilerParams(vmem_limit_bytes=limit << 20),
        cost_estimate=pl.CostEstimate(flops=flops, bytes_accessed=1 << 20, transcendentals=0),
    )(*ins)


def halves(value):
    high = value.astype(BF16)
    return high, (value - high.astype(F32)).astype(BF16)


def lane_groups(shape):
    return lax.broadcasted_iota(jnp.int32, shape, 1) // 32


def place(spots, b):
    pixels, strips, me = spots
    strip = strips[b]
    owner = strip >> 5
    slot = (((owner & 1) ^ me[1]) << 2) | (((owner >> 1) - me[0]) & 3)
    return (slot << 3) | ((strip >> 2) & 7), strip & 3, pixels[b]


def stacked(pair):
    high = pair[:, :128]
    return jnp.concatenate([pair, jnp.concatenate([high, jnp.zeros_like(high)], axis=1)], axis=0)


def forward_step(spots, g, pair, high, low, rays, groups):
    where = [place(spots, GROUP * g + i) for i in range(GROUP)]
    left = jnp.concatenate([jnp.concatenate([high[w[2]], low[w[2]]], axis=1) for w in where], axis=0)
    both = lax.dot_general(left, stacked(pair), (((1,), (0,)), ((), ())), preferred_element_type=F32)
    product = both[:, :128] + both[:, 128:]
    for i, (entry, spot, _) in enumerate(where):
        own = jnp.where(groups == i, product[32 * i : 32 * i + 32], 0.0)
        rays[entry] += pltpu.roll(own, ((spot - i) & 3) * 32, 1)


def forward_loop(spots, turned, high, low, rays):
    rays[...] = jnp.zeros_like(rays)
    groups = lane_groups((32, 128))

    def step(g, carry):
        forward_step(spots, g, turned[g], high, low, rays, groups)
        return carry

    lax.fori_loop(0, turned.shape[0], step, 0, unroll=UNROLL)


def back_loop(spots, plain, rays, field):
    field[...] = jnp.zeros_like(field)
    groups = lane_groups((32, 128))

    def step(g, carry):
        where = [place(spots, GROUP * g + i) for i in range(GROUP)]
        rows = []
        for i, (entry, spot, _) in enumerate(where):
            turned = pltpu.roll(rays[entry], ((i - spot) & 3) * 32, 1)
            own = jnp.where(groups == i, turned, 0.0)
            rows.append(jnp.concatenate(halves(own), axis=1))
        left = jnp.concatenate(rows, axis=0)
        both = lax.dot_general(
            left, stacked(plain[g]), (((1,), (0,)), ((), ())), preferred_element_type=F32
        )
        product = both[:, :128] + both[:, 128:]
        for i, (_, _, pixel) in enumerate(where):
            field[pixel] += product[32 * i : 32 * i + 32]
        return carry

    lax.fori_loop(0, plain.shape[0], step, 0, unroll=UNROLL)


def hand_out(rays, parts):
    for slot, part in enumerate(parts):
        part[...] = rays[8 * slot : 8 * slot + 8]


def first_kernel(pixels_hbm, strips_hbm, me, foot_hbm, volume_hbm, *refs):
    parts, (plain, turned, foot, volume, high, low, rays, pixels, strips, sem, foot_sem) = refs[:8], refs[8:]
    spots = (pixels, strips, me)
    per = foot.shape[0] // CHUNKS

    def chunk(t):
        some = pl.ds(t * per, per)
        return pltpu.make_async_copy(foot_hbm.at[some], foot.at[some], foot_sem.at[t])

    field = pltpu.make_async_copy(volume_hbm, volume, sem.at[0])
    field.start()
    indices = [
        pltpu.make_async_copy(pixels_hbm, pixels, sem.at[1]),
        pltpu.make_async_copy(strips_hbm, strips, sem.at[2]),
    ]
    for copy in indices:
        copy.start()
    for t in range(CHUNKS):
        chunk(t).start()
    rays[...] = jnp.zeros_like(rays)
    groups = lane_groups((32, 128))
    for copy in (*indices, field):
        copy.wait()
    for p in range(high.shape[0]):
        high[p], low[p] = halves(volume[:, 128 * p : 128 * p + 128])

    def trip(t, carry):
        chunk(t).wait()
        for u in range(per // GROUP):
            g = t * (per // GROUP) + u
            block = foot[pl.ds(GROUP * g, GROUP)].reshape(GROUP * 32, 128)
            plain[g] = jnp.concatenate(halves(block), axis=1)
            pair = jnp.concatenate(halves(block.T), axis=1)
            turned[g] = pair
            forward_step(spots, g, pair, high, low, rays, groups)
        return carry

    lax.fori_loop(0, CHUNKS, trip, 0)
    hand_out(rays, parts)


def folded(value):
    return jnp.sum(value.reshape(-1, 8, 128), axis=0)


def there_and_back(spots, plain, turned, pieces, parts, field, high, low, rays):
    for slot, piece in enumerate(pieces):
        rays[8 * slot : 8 * slot + 8] = piece[...]
    back_loop(spots, plain, rays, field)
    for p in range(high.shape[0]):
        high[p], low[p] = halves(field[p])
    forward_loop(spots, turned, high, low, rays)
    hand_out(rays, parts)


def second_kernel(pixels, strips, me, plain, turned, *refs):
    pieces, parts, (field, sums, high, low, rays) = refs[:8], refs[8:16], refs[16:]
    there_and_back((pixels, strips, me), plain, turned, pieces, parts, field, high, low, rays)
    sums[0] = folded(field[...] * field[...])


def third_kernel(pixels, strips, me, plain, turned, *refs):
    pieces, grad, parts = refs[:8], refs[8], refs[9:17]
    field, sums, first, last, high, low, rays = refs[17:]
    there_and_back((pixels, strips, me), plain, turned, pieces, parts, field, high, low, rays)
    sums[0] = folded(grad[...] * field[...])
    sums[1] = folded(field[...] * field[...])
    row = lax.broadcasted_iota(jnp.int32, (8, 128), 0)
    for p in range(field.shape[0]):
        first[p] = jnp.where(row < 3, grad[p, 0:8], pltpu.roll(field[p, 0:8], 3, 0))
        last[p] = jnp.where(row > 4, grad[p, 24:32], pltpu.roll(field[p, 24:32], 5, 0))


def add_kernel(one, other, out):
    out[...] = one[...] + other[...]


def tile_cols(ref):
    return jnp.stack([ref[:, 128 * t : 128 * t + 128] for t in range(ref.shape[1] // 128)])


def start_kernel(own, got, a, b, c, measured, weights, residual, sent):
    value = own[...] + got[...] + a[...] + b[...] + c[...] - tile_cols(measured)
    residual[...] = value
    sent[...] = tile_cols(weights) * value


def middle_kernel(own, got, a, b, c, weights, projected, sent, sums):
    value = own[...] + got[...] + a[...] + b[...] + c[...]
    weighted = tile_cols(weights) * value
    projected[...] = value
    sent[...] = weighted
    sums[0] = folded(weighted * value)


def in_lanes(sums, shape):
    lane = lax.broadcasted_iota(jnp.int32, shape, 1)
    value = jnp.zeros(shape, F32)
    for n, part in enumerate(sums):
        value = jnp.where(lane == n, jnp.sum(part, keepdims=True), value)
    return value


def end_kernel(own, got, a, b, c, weights, before, norm0, curve0, turned, projected, sums):
    value = own[...] + got[...] + a[...] + b[...] + c[...]
    weighted = tile_cols(weights) * value
    projected[...] = value
    cross = folded(weighted * before[...])
    sums[...] = in_lanes([norm0[0], curve0[0], turned[0], turned[1], cross, folded(weighted * value)], sums.shape)


def totals(rows, count):
    value = jnp.sum(rows[...], axis=0, keepdims=True)
    return [jnp.sum(value[:, n : n + 1]) for n in range(count)]


def judge_kernel(rows, alphas, again):
    norm0, curve0, cross_g, square_g, cross_p, square_p = totals(rows, 6)
    alpha = norm0 / curve0
    norm1 = norm0 - 2.0 * alpha * cross_g + alpha * alpha * square_g
    curve1 = curve0 - 2.0 * alpha * cross_p + alpha * alpha * square_p
    sound = (norm1 > 0.01 * norm0) & (curve1 > 0.01 * curve0)
    for square in (square_g, square_p):
        sound = sound & (square > 1e-25) & (square < 1e37)
    alphas[0] = alpha
    alphas[1] = norm1 / curve1
    again[0] = jnp.where(sound, 0, 1)


def again_kernel(alphas, weights, p0, q0, grad, turned, sums):
    value = p0[...] - alphas[0] * q0[...]
    step = grad[...] - alphas[0] * turned[...]
    sums[...] = in_lanes([folded(step * step), folded(tile_cols(weights) * value * value)], sums.shape)


def spread_kernel(own, got, rows):
    rows[...] = jnp.broadcast_to(own[0:1] + got[0:1], rows.shape)


def ratio_kernel(alphas, rows, out):
    norm1, curve1 = totals(rows, 2)
    out[0] = alphas[0]
    out[1] = norm1 / curve1


def smooth_kernel(ends, alphas, volume, grad, turned, first0, last0, first, last, residual, p0, q0, smoothed, left_over):
    alpha0, alpha1 = alphas[0], alphas[1]
    rest = residual[...] - alpha0 * p0[...] - alpha1 * (p0[...] - alpha0 * q0[...])
    for t in range(rest.shape[0]):
        left_over[:, 128 * t : 128 * t + 128] = rest[t]

    def stepped(x, g, h):
        return x - alpha0 * g - alpha1 * (g - alpha0 * h)

    row = lax.broadcasted_iota(jnp.int32, (48, 128), 0)
    open_link = ~(((row == 7) & (ends[0] == 1)) | ((row == 39) & (ends[1] == 1)))
    link = jnp.where(open_link, F32(1.0), F32(0.0))
    for p in range(grad.shape[0]):
        cols = slice(128 * p, 128 * p + 128)
        ext = jnp.concatenate(
            [
                stepped(last0[:, cols], last[p], pltpu.roll(last[p], 3, 0)),
                stepped(volume[:, cols], grad[p], turned[p]),
                stepped(first0[:, cols], first[p], pltpu.roll(first[p], 5, 0)),
            ],
            axis=0,
        )
        for _ in range(PASSES):
            clipped = jnp.clip(pltpu.roll(ext, 47, 0) - ext, -huber_width, huber_width) * link
            ext = ext + smooth_rate * (clipped - pltpu.roll(clipped, 1, 0))
        smoothed[:, cols] = ext[8:40]


def shift(value, axis, by):
    n = lax.axis_size(axis)
    return lax.ppermute(value, axis, [(i, (i + by) % n) for i in range(n)])


RAY = (8, 32, 128)


def summed_by_owner(parts):
    own, theirs = parts[:4], parts[4:8]
    got, moved = {}, {}
    for r in (2, 1, 3, 0):
        got[r] = shift(theirs[r], "tile_1", 1)
    for r in (2, 1, 3):
        part = call(add_kernel, [RAY], [own[r], got[r]])[0]
        moved[r] = shift(part, "tile_0", r)
    return own[0], got[0], moved[1], moved[2], moved[3]


def to_everyone(own):
    column = [own] + [shift(own, "tile_0", -r) for r in (1, 2, 3)]
    return column + [shift(block, "tile_1", 1) for block in column]


def over_all(sums):
    got = shift(sums, "tile_1", 1)
    axes = ("tile_0",) + SLAB
    rows = call(spread_kernel, [(lax.axis_size(axes), 128)], [sums, got])[0]
    return lax.all_to_all(rows, axes, 0, 0, tiled=True)


def shards(volume, measured, weights, footprints, foot_pixel, foot_strip):
    me = jnp.stack([lax.axis_index("tile_0"), lax.axis_index("tile_1")])
    spots = [foot_pixel, foot_strip, me]
    slabs = lax.axis_size(SLAB)
    place_in = lax.axis_index(SLAB)
    ends = jnp.stack([place_in == 0, place_in == slabs - 1]).astype(jnp.int32)
    up = [(i, i + 1) for i in range(slabs - 1)]
    down = [(j, i) for i, j in up]

    field, tile = (32, 32, 128), (1, 8, 128)
    scratch = [pltpu.VMEM(field, BF16), pltpu.VMEM(field, BF16), pltpu.VMEM((64, 32, 128), F32)]
    streams = [
        pltpu.VMEM(footprints.shape, F32),
        pltpu.VMEM(volume.shape, F32),
        *scratch,
        pltpu.SMEM(foot_pixel.shape, jnp.int32),
        pltpu.SMEM(foot_strip.shape, jnp.int32),
        pltpu.SemaphoreType.DMA((3,)),
        pltpu.SemaphoreType.DMA((CHUNKS,)),
    ]
    split = jax.ShapeDtypeStruct((64, 128, 256), BF16)
    *parts, plain, turned = call(
        first_kernel,
        [RAY] * 8 + [split, split],
        [*spots, footprints, volume],
        streams,
        3,
        any_at=(0, 1, 3, 4),
        limit=32,
    )
    last0 = lax.ppermute(volume[24:32], SLAB, up)
    first0 = lax.ppermute(volume[0:8], SLAB, down)
    parts = summed_by_owner(parts)
    residual, sent = call(start_kernel, [RAY, RAY], [*parts, measured, weights])

    *parts, grad, norm0 = call(
        second_kernel, [RAY] * 8 + [field, tile], [*spots, plain, turned, *to_everyone(sent)], scratch, 3
    )
    parts = summed_by_owner(parts)
    p0, sent, curve0 = call(middle_kernel, [RAY, RAY, tile], [*parts, weights])

    edge = (32, 8, 128)
    *parts, back, crossed, first, last = call(
        third_kernel,
        [RAY] * 8 + [field, (2, 8, 128), edge, edge],
        [*spots, plain, turned, *to_everyone(sent), grad],
        scratch,
        3,
    )
    last = lax.ppermute(last, SLAB, up)
    first = lax.ppermute(first, SLAB, down)
    parts = summed_by_owner(parts)
    q0, sums = call(end_kernel, [RAY, (8, 128)], [*parts, weights, p0, norm0, curve0, crossed])
    rows = over_all(sums)
    alphas, again = pl.pallas_call(
        judge_kernel,
        out_shape=[jax.ShapeDtypeStruct((2,), F32), jax.ShapeDtypeStruct((1,), jnp.int32)],
        in_specs=[VM],
        out_specs=[SM, SM],
        compiler_params=pltpu.CompilerParams(vmem_limit_bytes=8 << 20),
    )(rows)

    def summed_again(alphas):
        sums = call(again_kernel, [(8, 128)], [alphas, weights, p0, q0, grad, back], (), 1)[0]
        return pl.pallas_call(
            ratio_kernel,
            out_shape=jax.ShapeDtypeStruct((2,), F32),
            in_specs=[SM, VM],
            out_specs=SM,
            compiler_params=pltpu.CompilerParams(vmem_limit_bytes=8 << 20),
        )(alphas, over_all(sums))

    alphas = lax.cond(again[0] == 1, summed_again, lambda known: known, alphas)
    return call(
        smooth_kernel,
        [volume.shape, measured.shape],
        [ends, alphas, volume, grad, back, first0, last0, first, last, residual, p0, q0],
        (),
        2,
    )


def solution(mesh):
    finer = Mesh(mesh.devices.reshape(4, 2, 4, 4), ("tile_0", "tile_1", "slab_0", "slab_1"))
    return jax.shard_map(
        lambda *args: tuple(shards(*args)),
        mesh=finer,
        in_specs=(
            P(SLAB, TILE),
            P(SLAB, TILE),
            P(SLAB, TILE),
            P(TILE, None, None),
            P(TILE),
            P(TILE),
        ),
        out_specs=(P(SLAB, TILE), P(SLAB, TILE)),
        check_vma=False,
    )
```

time: 116 us -> 119 us (1.026)
  starting transfers between devices: 52 us -> 56.1 us
  Pallas kernels: 23.8 us -> 21.3 us
  local copies, waits for them, and re-layouts: 3.24 us -> 4.62 us
    ppermute x0 -> x2, starting transfers between devices: none -> 5.29 us  [the longest x1 3.99 us: shards(): last0 = lax.ppermute(volume[24:32], SLAB, up)]
    ppermute x26 -> x36, starting transfers between devices: 33.7 us -> 30 us  [shift(): return lax.ppermute(value, axis, [(i, (i + by) % n) for i in range(n)])]
    all_to_all x1, starting transfers between devices: 13 us -> 15.5 us  [over_all(): return lax.all_to_all(rows, axes, 0, 0, tiled=True)]
    pallas_call x10 -> x17, Pallas kernels: 23 us -> 20.5 us  [call(): pl.pallas_call(kernel, out_shape=[s if hasattr(s, 'dtype') else jax.Shape...]
    ppermute x26 -> x36, waiting for transfers between devices: 24.5 us -> 26.4 us  [shift(): return lax.ppermute(value, axis, [(i, (i + by) % n) for i in range(n)])]
    all_to_all x1, waiting for transfers between devices: 9.66 us -> 8.28 us  [over_all(): return lax.all_to_all(rows, axes, 0, 0, tiled=True)]
    unnamed x14, local copies, waits for them, and re-layouts: 3.24 us -> 4.6 us
  transfers between devices with their start and end apart: 29 -> 41, of which waited for: 15 -> 17; matrix products, arithmetic and copies ran while one was open for 0% -> 0% of each run, Pallas kernels for 1% -> 1%
where the time goes in v1:
time: 119 us; the launch traced here: 118 us
  starting transfers between devices  56.1 us (47%)
  waiting for transfers between devices  34.6 us (29%)
  Pallas kernels  21.3 us (18%)
  local copies, waits for them, and re-layouts  4.62 us (4%)
  between operations  1.56 us (1%)
    ppermute x36, starting transfers between devices, shift(): return lax.ppermute(value, axis, [(i, (i + by) % n) for i in range(n)])  30 us
    ppermute x36, waiting for transfers between devices, shift(): return lax.ppermute(value, axis, [(i, (i + by) % n) for i in range(n)])  26.4 us
    pallas_call x17, Pallas kernels, call(): pl.pallas_call(kernel, out_shape=[s if hasattr(s, 'dtype') else jax.Shape...  20.5 us
    all_to_all x1, starting transfers between devices, over_all(): return lax.all_to_all(rows, axes, 0, 0, tiled=True)  15.5 us
    all_to_all x1, waiting for transfers between devices, over_all(): return lax.all_to_all(rows, axes, 0, 0, tiled=True)  8.28 us
    unnamed x14, local copies, waits for them, and re-layouts  4.6 us
    ppermute x1, starting transfers between devices, shards(): last = lax.ppermute(last, SLAB, up)  3.99 us
    ppermute x1, starting transfers between devices, shards(): last0 = lax.ppermute(volume[24:32], SLAB, up)  3.99 us
  transfers between devices with their start and end apart: 41, of which 17 were waited for; matrix products, arithmetic and copies ran while one was open for 0% of the time, Pallas kernels for 1%

profile of v1, /device:TPU:1, one launch (start us, length us, event | category | flops | bytes accessed | tf_op | source)
XLA Modules:
  0.0 118.4 jit_solution(9850431178583928556)
XLA Ops:
  0.7 2.2 %copy-done = f32[256,32,128]{2,1,0:T(8,128)S(1)} copy-done((f32[256,32,128]{2,1,0:T(8,128)S(1)}, f32[256,32,128]{2,1,0:T(8,128)}, u32[]{:S(2)}) %copy-start) | copy-done | bytes 4194328
  5.3 5.0 %shard_map.77 = (f32[8,32,128]{2,1,0:T(8,128)S(1)}, f32[8,32,128]{2,1,0:T(8,128)S(1)}, f32[8,32,128]{2,1,0:T(8,128)S(1)}, f32[8,32,128]{2,1,0:T(8,128)S(1)}, f32...) custom-call(s32[256]{0:T(256)S(1)} %copy-done.4, ...), custom_call_target="tpu_custom_call" | custom-call | flops 1000000 | bytes 1048576 | tf_op jit(solution)/shard_map/pallas_call | solution.py:29
  10.3 1.5 %collective-permute-start.6 = (f32[8,32,128]{2,1,0:T(8,128)S(1)}, f32[8,32,128]{2,1,0:T(8,128)S(1)}, u32[]{:S(2)}, u32[]{:S(2)}) collective-permute-start(f32[8,32,128]{2,1,0:T(8,128)S(1)} %get-tuple-element.74), channel_id=1, source_target_pairs={{0,16},{16,0},{1,17},{17,1},{2,18},{18,2},{3,19},{19,3},{4,20},{20... | collective-permute-start | bytes 393224 | tf_op jit(solution)/shard_map/ppermute | solution.py:286
  12.7 2.9 %collective-permute-start.7 = (f32[8,32,128]{2,1,0:T(8,128)S(1)}, f32[8,32,128]{2,1,0:T(8,128)S(1)}, u32[]{:S(2)}, u32[]{:S(2)}) collective-permute-start(f32[8,32,128]{2,1,0:T(8,128)S(1)} %shard_map.80), channel_id=1, source_target_pairs={{0,96},{32,0},{64,32},{96,64},{1,97},{33,1},{65,33},{97,65},{2,98}... | collective-permute-start | bytes 393224 | tf_op jit(solution)/shard_map/ppermute | solution.py:286
  16.9 3.9 %collective-permute-done.7.c = f32[8,32,128]{2,1,0:T(8,128)S(1)} collective-permute-done((f32[8,32,128]{2,1,0:T(8,128)S(1)}, f32[8,32,128]{2,1,0:T(8,128)S(1)}, u32[]{:S(2)}, u32[]{:S(2)}) %collective-permute-start.7) | collective-permute-done | bytes 131104 | tf_op jit(solution)/shard_map/ppermute | solution.py:286
  21.7 3.8 %collective-permute-done.3.a = f32[8,32,128]{2,1,0:T(8,128)S(1)} collective-permute-done((f32[8,32,128]{2,1,0:T(8,128)S(1)}, f32[8,32,128]{2,1,0:T(8,128)S(1)}, u32[]{:S(2)}, u32[]{:S(2)}) %collective-permute-start.3) | collective-permute-done | bytes 131104 | tf_op jit(solution)/shard_map/ppermute | solution.py:286
  25.9 1.2 collective-permute-start.10
  27.1 1.2 collective-permute-start.11
  28.3 1.9 %collective-permute-done.8.refs_1_ = f32[8,32,128]{2,1,0:T(8,128)S(1)} collective-permute-done((f32[8,32,128]{2,1,0:T(8,128)S(1)}, f32[8,32,128]{2,1,0:T(8,128)S(1)}, u32[]{:S(2)}, u32[]{:S(2)}) %collective-permute-start.8) | collective-permute-done | bytes 131104 | tf_op jit(solution)/shard_map/ppermute | solution.py:286
  30.2 2.3 %collective-permute-start.12 = (f32[8,32,128]{2,1,0:T(8,128)S(1)}, f32[8,32,128]{2,1,0:T(8,128)S(1)}, u32[]{:S(2)}, u32[]{:S(2)}) collective-permute-start(f32[8,32,128]{2,1,0:T(8,128)S(1)} %collective-permute-done.8.refs_1_), channel_id=1, source_target_pairs={{0,16},{16,0},{1,17},{17,1},{2,18},{18,2},{3,19},{19,3},{4,20},{20... | collective-permute-start | bytes 393224 | tf_op jit(solution)/shard_map/ppermute | solution.py:286
  32.5 1.5 %collective-permute-start.13 = (f32[8,32,128]{2,1,0:T(8,128)S(1)}, f32[8,32,128]{2,1,0:T(8,128)S(1)}, u32[]{:S(2)}, u32[]{:S(2)}) collective-permute-start(f32[8,32,128]{2,1,0:T(8,128)S(1)} %collective-permute-done.9.refs_2_), channel_id=1, source_target_pairs={{0,16},{16,0},{1,17},{17,1},{2,18},{18,2},{3,19},{19,3},{4,20},{20... | collective-permute-start | bytes 393224 | tf_op jit(solution)/shard_map/ppermute | solution.py:286
  34.0 1.4 %collective-permute-done.10.refs_3_ = f32[8,32,128]{2,1,0:T(8,128)S(1)} collective-permute-done((f32[8,32,128]{2,1,0:T(8,128)S(1)}, f32[8,32,128]{2,1,0:T(8,128)S(1)}, u32[]{:S(2)}, u32[]{:S(2)}) %collective-permute-start.10) | collective-permute-done | bytes 131104 | tf_op jit(solution)/shard_map/ppermute | solution.py:286
  36.9 6.1 %shard_map.82 = (f32[8,32,128]{2,1,0:T(8,128)S(1)}, f32[8,32,128]{2,1,0:T(8,128)S(1)}, f32[8,32,128]{2,1,0:T(8,128)S(1)}, f32[8,32,128]{2,1,0:T(8,128)S(1)}, f32...) custom-call(s32[256]{0:T(256)S(1)} %copy-done.4, ...), custom_call_target="tpu_custom_call" | custom-call | flops 1000000 | bytes 1048576 | tf_op jit(solution)/shard_map/pallas_call | solution.py:29
  44.5 1.2 %collective-permute-start.21 = (f32[8,32,128]{2,1,0:T(8,128)S(1)}, f32[8,32,128]{2,1,0:T(8,128)S(1)}, u32[]{:S(2)}, u32[]{:S(2)}) collective-permute-start(f32[8,32,128]{2,1,0:T(8,128)S(1)} %shard_map.85), channel_id=1, source_target_pairs={{0,96},{32,0},{64,32},{96,64},{1,97},{33,1},{65,33},{97,65},{2,98}... | collective-permute-start | bytes 393224 | tf_op jit(solution)/shard_map/ppermute | solution.py:286
  46.6 2.7 %collective-permute-done.21.c = f32[8,32,128]{2,1,0:T(8,128)S(1)} collective-permute-done((f32[8,32,128]{2,1,0:T(8,128)S(1)}, f32[8,32,128]{2,1,0:T(8,128)S(1)}, u32[]{:S(2)}, u32[]{:S(2)}) %collective-permute-start.21) | collective-permute-done | bytes 131104 | tf_op jit(solution)/shard_map/ppermute | solution.py:286
  49.3 2.7 %collective-permute-done.19.b = f32[8,32,128]{2,1,0:T(8,128)S(1)} collective-permute-done((f32[8,32,128]{2,1,0:T(8,128)S(1)}, f32[8,32,128]{2,1,0:T(8,128)S(1)}, u32[]{:S(2)}, u32[]{:S(2)}) %collective-permute-start.19) | collective-permute-done | bytes 131104 | tf_op jit(solution)/shard_map/ppermute | solution.py:286
  52.0 3.2 %collective-permute-done.17.a = f32[8,32,128]{2,1,0:T(8,128)S(1)} collective-permute-done((f32[8,32,128]{2,1,0:T(8,128)S(1)}, f32[8,32,128]{2,1,0:T(8,128)S(1)}, u32[]{:S(2)}, u32[]{:S(2)}) %collective-permute-start.17) | collective-permute-done | bytes 131104 | tf_op jit(solution)/shard_map/ppermute | solution.py:286
  55.6 1.2 %collective-permute-start.24 = (f32[8,32,128]{2,1,0:T(8,128)S(1)}, f32[8,32,128]{2,1,0:T(8,128)S(1)}, u32[]{:S(2)}, u32[]{:S(2)}) collective-permute-start(f32[8,32,128]{2,1,0:T(8,128)S(1)} %get-tuple-element.84.refs_0_), channel_id=1, source_target_pairs={{0,32},{32,64},{64,96},{96,0},{1,33},{33,65},{65,97},{97,1},{2,34}... | collective-permute-start | bytes 393224 | tf_op jit(solution)/shard_map/ppermute | solution.py:286
  56.8 1.2 %collective-permute-start.25 = (f32[8,32,128]{2,1,0:T(8,128)S(1)}, f32[8,32,128]{2,1,0:T(8,128)S(1)}, u32[]{:S(2)}, u32[]{:S(2)}) collective-permute-start(f32[8,32,128]{2,1,0:T(8,128)S(1)} %get-tuple-element.84.refs_0_), channel_id=1, source_target_pairs={{0,16},{16,0},{1,17},{17,1},{2,18},{18,2},{3,19},{19,3},{4,20},{20... | collective-permute-start | bytes 393224 | tf_op jit(solution)/shard_map/ppermute | solution.py:286
  58.0 1.7 %collective-permute-done.22.refs_1_ = f32[8,32,128]{2,1,0:T(8,128)S(1)} collective-permute-done((f32[8,32,128]{2,1,0:T(8,128)S(1)}, f32[8,32,128]{2,1,0:T(8,128)S(1)}, u32[]{:S(2)}, u32[]{:S(2)}) %collective-permute-start.22) | collective-permute-done | bytes 131104 | tf_op jit(solution)/shard_map/ppermute | solution.py:286
  59.7 2.6 %collective-permute-start.26 = (f32[8,32,128]{2,1,0:T(8,128)S(1)}, f32[8,32,128]{2,1,0:T(8,128)S(1)}, u32[]{:S(2)}, u32[]{:S(2)}) collective-permute-start(f32[8,32,128]{2,1,0:T(8,128)S(1)} %collective-permute-done.22.refs_1_), channel_id=1, source_target_pairs={{0,16},{16,0},{1,17},{17,1},{2,18},{18,2},{3,19},{19,3},{4,20},{20... | collective-permute-start | bytes 393224 | tf_op jit(solution)/shard_map/ppermute | solution.py:286
  62.4 2.1 %collective-permute-start.27 = (f32[8,32,128]{2,1,0:T(8,128)S(1)}, f32[8,32,128]{2,1,0:T(8,128)S(1)}, u32[]{:S(2)}, u32[]{:S(2)}) collective-permute-start(f32[8,32,128]{2,1,0:T(8,128)S(1)} %collective-permute-done.23.refs_2_), channel_id=1, source_target_pairs={{0,16},{16,0},{1,17},{17,1},{2,18},{18,2},{3,19},{19,3},{4,20},{20... | collective-permute-start | bytes 393224 | tf_op jit(solution)/shard_map/ppermute | solution.py:286
  66.7 6.2 %shard_map.87 = (f32[8,32,128]{2,1,0:T(8,128)S(1)}, f32[8,32,128]{2,1,0:T(8,128)S(1)}, f32[8,32,128]{2,1,0:T(8,128)S(1)}, f32[8,32,128]{2,1,0:T(8,128)S(1)}, f32...) custom-call(s32[256]{0:T(256)S(1)} %copy-done.4, ...), custom_call_target="tpu_custom_call" | custom-call | flops 1000000 | bytes 1048576 | tf_op jit(solution)/shard_map/pallas_call | solution.py:29
  74.3 1.2 %collective-permute-start.35 = (f32[8,32,128]{2,1,0:T(8,128)S(1)}, f32[8,32,128]{2,1,0:T(8,128)S(1)}, u32[]{:S(2)}, u32[]{:S(2)}) collective-permute-start(f32[8,32,128]{2,1,0:T(8,128)S(1)} %shard_map.90), channel_id=1, source_target_pairs={{0,96},{32,0},{64,32},{96,64},{1,97},{33,1},{65,33},{97,65},{2,98}... | collective-permute-start | bytes 393224 | tf_op jit(solution)/shard_map/ppermute | solution.py:286
  76.4 1.3 %collective-permute-start.37 = (f32[8,4096]{1,0:T(8,128)S(1)}, f32[8,4096]{1,0:T(8,128)S(1)}, u32[]{:S(2)}, u32[]{:S(2)}) collective-permute-start(f32[8,4096]{1,0:T(8,128)S(1)} %get-tuple-element.107), channel_id=1, source_target_pairs={{1,0},{2,1},{3,2},{4,3},{5,4},{6,5},{7,6},{8,7},{9,8},{10,9},{11,1... | collective-permute-start | bytes 393224 | tf_op jit(solution)/shard_map/ppermute | solution.py:346
  77.7 4.0 %collective-permute-start.38 = (f32[8,4096]{1,0:T(8,128)S(1)}, f32[8,4096]{1,0:T(8,128)S(1)}, u32[]{:S(2)}, u32[]{:S(2)}) collective-permute-start(f32[8,4096]{1,0:T(8,128)S(1)} %get-tuple-element.106), channel_id=1, source_target_pairs={{0,1},{1,2},{2,3},{3,4},{4,5},{5,6},{6,7},{7,8},{8,9},{9,10},{10,1... | collective-permute-start | bytes 393224 | tf_op jit(solution)/shard_map/ppermute | solution.py:345
  81.7 1.3 %collective-permute-start.39 = (f32[32,8,128]{2,1,0:T(8,128)S(1)}, f32[32,8,128]{2,1,0:T(8,128)S(1)}, u32[]{:S(2)}, u32[]{:S(2)}) collective-permute-start(f32[32,8,128]{2,1,0:T(8,128)S(1)} %get-tuple-element.103), channel_id=1, source_target_pairs={{1,0},{2,1},{3,2},{4,3},{5,4},{6,5},{7,6},{8,7},{9,8},{10,9},{11,1... | collective-permute-start | bytes 393224 | tf_op jit(solution)/shard_map/ppermute | solution.py:365
  83.0 4.0 %collective-permute-start.40 = (f32[32,8,128]{2,1,0:T(8,128)S(1)}, f32[32,8,128]{2,1,0:T(8,128)S(1)}, u32[]{:S(2)}, u32[]{:S(2)}) collective-permute-start(f32[32,8,128]{2,1,0:T(8,128)S(1)} %get-tuple-element.104), channel_id=1, source_target_pairs={{0,1},{1,2},{2,3},{3,4},{4,5},{5,6},{6,7},{7,8},{8,9},{9,10},{10,1... | collective-permute-start | bytes 393224 | tf_op jit(solution)/shard_map/ppermute | solution.py:364
  87.2 2.1 %collective-permute-start.36 = (f32[8,128]{1,0:T(8,128)S(1)}, f32[8,128]{1,0:T(8,128)S(1)}, u32[]{:S(2)}, u32[]{:S(2)}) collective-permute-start(f32[8,128]{1,0:T(8,128)S(1)} %get-tuple-element.98.own), channel_id=1, source_target_pairs={{0,16},{16,0},{1,17},{17,1},{2,18},{18,2},{3,19},{19,3},{4,20},{20... | collective-permute-start | bytes 12296 | tf_op jit(solution)/shard_map/ppermute | solution.py:286
  90.8 15.5 %all-to-all-start.1 = ((f32[64,1,128]{2,1,0:T(1,128)}), f32[64,1,128]{2,1,0:T(1,128)S(1)}, u32[]{:S(2)}, u32[]{:S(2)}) async-start(f32[64,1,128]{2,1,0:T(1,128)} %bitcast.9), calls=%async_computation.1 | async-start | bytes 65536 | tf_op jit(solution)/shard_map/all_to_all | solution.py:312
  106.4 8.3 %all-to-all-done.1 = f32[64,1,128]{2,1,0:T(1,128)S(1)} async-done(((f32[64,1,128]{2,1,0:T(1,128)}), f32[64,1,128]{2,1,0:T(1,128)S(1)}, u32[]{:S(2)}, u32[]{:S(2)}) %all-to-all-start.1) | async-done | bytes 32800 | tf_op jit(solution)/shard_map/all_to_all | solution.py:312
  116.2 2.2 %shard_map.94 = (f32[32,4096]{1,0:T(8,128)}, f32[32,1024]{1,0:T(8,128)}) custom-call(s32[2]{0:T(128)S(1)} %add_convert_fusion.ends, f32[2]{0:T(128)S(1)} %get-tuple-element.108.alphas, f32[32,4096]{1,0:T(8,128)S(1)} %copy-done.2, f32[32,32,128]{2,1,0:T(8,128)S(1)} %get-tuple-element.85.refs_8_.grad, f32[32,32,128]{2,1,0:T(8,128)S(1)} %get-tuple-element.102.turned, ...), custom_call_target="tpu_custom_call" | custom-call | flops 1000000 | bytes 1048576 | tf_op jit(solution)/shard_map/pallas_call | solution.py:29
  (86 shorter events, 17.1 us)
Async XLA Ops:
  11.7 3.9 %collective-permute-start.4 = (f32[8,32,128]{2,1,0:T(8,128)S(1)}, f32[8,32,128]{2,1,0:T(8,128)S(1)}, u32[]{:S(2)}, u32[]{:S(2)}) collective-permute-start(f32[8,32,128]{2,1,0:T(8,128)S(1)} %get-tuple-element.72), channel_id=1, source_target_pairs={{0,16},{16,0},{1,17},{17,1},{2,18},{18,2},{3,19},{19,3},{4,20},{20... | collective-permute-start | bytes 393224 | tf_op jit(solution)/shard_map/ppermute | solution.py:286
  11.8 4.4 %collective-permute-start.2 = (f32[8,32,128]{2,1,0:T(8,128)S(1)}, f32[8,32,128]{2,1,0:T(8,128)S(1)}, u32[]{:S(2)}, u32[]{:S(2)}) collective-permute-start(f32[8,32,128]{2,1,0:T(8,128)S(1)} %get-tuple-element.70), channel_id=1, source_target_pairs={{0,16},{16,0},{1,17},{17,1},{2,18},{18,2},{3,19},{19,3},{4,20},{20... | collective-permute-start | bytes 393224 | tf_op jit(solution)/shard_map/ppermute | solution.py:286
  12.2 4.6 %collective-permute-start.1 = (f32[8,32,128]{2,1,0:T(8,128)S(1)}, f32[8,32,128]{2,1,0:T(8,128)S(1)}, u32[]{:S(2)}, u32[]{:S(2)}) collective-permute-start(f32[8,32,128]{2,1,0:T(8,128)S(1)} %get-tuple-element.68), channel_id=1, source_target_pairs={{0,16},{16,0},{1,17},{17,1},{2,18},{18,2},{3,19},{19,3},{4,20},{20... | collective-permute-start | bytes 393224 | tf_op jit(solution)/shard_map/ppermute | solution.py:286
  12.7 8.1 %collective-permute-start.7 = (f32[8,32,128]{2,1,0:T(8,128)S(1)}, f32[8,32,128]{2,1,0:T(8,128)S(1)}, u32[]{:S(2)}, u32[]{:S(2)}) collective-permute-start(f32[8,32,128]{2,1,0:T(8,128)S(1)} %shard_map.80), channel_id=1, source_target_pairs={{0,96},{32,0},{64,32},{96,64},{1,97},{33,1},{65,33},{97,65},{2,98}... | collective-permute-start | bytes 393224 | tf_op jit(solution)/shard_map/ppermute | solution.py:286
  15.7 6.0 %collective-permute-start.5 = (f32[8,32,128]{2,1,0:T(8,128)S(1)}, f32[8,32,128]{2,1,0:T(8,128)S(1)}, u32[]{:S(2)}, u32[]{:S(2)}) collective-permute-start(f32[8,32,128]{2,1,0:T(8,128)S(1)} %shard_map.79), channel_id=1, source_target_pairs={{0,64},{32,96},{64,0},{96,32},{1,65},{33,97},{65,1},{97,33},{2,66}... | collective-permute-start | bytes 393224 | tf_op jit(solution)/shard_map/ppermute | solution.py:286
  16.2 9.3 %collective-permute-start.3 = (f32[8,32,128]{2,1,0:T(8,128)S(1)}, f32[8,32,128]{2,1,0:T(8,128)S(1)}, u32[]{:S(2)}, u32[]{:S(2)}) collective-permute-start(f32[8,32,128]{2,1,0:T(8,128)S(1)} %shard_map.78), channel_id=1, source_target_pairs={{0,32},{32,64},{64,96},{96,0},{1,33},{33,65},{65,97},{97,1},{2,34}... | collective-permute-start | bytes 393224 | tf_op jit(solution)/shard_map/ppermute | solution.py:286
  25.6 4.6 %collective-permute-start.8 = (f32[8,32,128]{2,1,0:T(8,128)S(1)}, f32[8,32,128]{2,1,0:T(8,128)S(1)}, u32[]{:S(2)}, u32[]{:S(2)}) collective-permute-start(f32[8,32,128]{2,1,0:T(8,128)S(1)} %get-tuple-element.75.refs_0_), channel_id=1, source_target_pairs={{0,96},{32,0},{64,32},{96,64},{1,97},{33,1},{65,33},{97,65},{2,98}... | collective-permute-start | bytes 393224 | tf_op jit(solution)/shard_map/ppermute | solution.py:286
  25.6 6.9 %collective-permute-start.9 = (f32[8,32,128]{2,1,0:T(8,128)S(1)}, f32[8,32,128]{2,1,0:T(8,128)S(1)}, u32[]{:S(2)}, u32[]{:S(2)}) collective-permute-start(f32[8,32,128]{2,1,0:T(8,128)S(1)} %get-tuple-element.75.refs_0_), channel_id=1, source_target_pairs={{0,64},{32,96},{64,0},{96,32},{1,65},{33,97},{65,1},{97,33},{2,66}... | collective-permute-start | bytes 393224 | tf_op jit(solution)/shard_map/ppermute | solution.py:286
  25.9 9.5 %collective-permute-start.10 = (f32[8,32,128]{2,1,0:T(8,128)S(1)}, f32[8,32,128]{2,1,0:T(8,128)S(1)}, u32[]{:S(2)}, u32[]{:S(2)}) collective-permute-start(f32[8,32,128]{2,1,0:T(8,128)S(1)} %get-tuple-element.75.refs_0_), channel_id=1, source_target_pairs={{0,32},{32,64},{64,96},{96,0},{1,33},{33,65},{65,97},{97,1},{2,34}... | collective-permute-start | bytes 393224 | tf_op jit(solution)/shard_map/ppermute | solution.py:286
  27.1 8.9 %collective-permute-start.11 = (f32[8,32,128]{2,1,0:T(8,128)S(1)}, f32[8,32,128]{2,1,0:T(8,128)S(1)}, u32[]{:S(2)}, u32[]{:S(2)}) collective-permute-start(f32[8,32,128]{2,1,0:T(8,128)S(1)} %get-tuple-element.75.refs_0_), channel_id=1, source_target_pairs={{0,16},{16,0},{1,17},{17,1},{2,18},{18,2},{3,19},{19,3},{4,20},{20... | collective-permute-start | bytes 393224 | tf_op jit(solution)/shard_map/ppermute | solution.py:286
  30.2 5.8 %collective-permute-start.12 = (f32[8,32,128]{2,1,0:T(8,128)S(1)}, f32[8,32,128]{2,1,0:T(8,128)S(1)}, u32[]{:S(2)}, u32[]{:S(2)}) collective-permute-start(f32[8,32,128]{2,1,0:T(8,128)S(1)} %collective-permute-done.8.refs_1_), channel_id=1, source_target_pairs={{0,16},{16,0},{1,17},{17,1},{2,18},{18,2},{3,19},{19,3},{4,20},{20... | collective-permute-start | bytes 393224 | tf_op jit(solution)/shard_map/ppermute | solution.py:286
  32.5 3.5 %collective-permute-start.13 = (f32[8,32,128]{2,1,0:T(8,128)S(1)}, f32[8,32,128]{2,1,0:T(8,128)S(1)}, u32[]{:S(2)}, u32[]{:S(2)}) collective-permute-start(f32[8,32,128]{2,1,0:T(8,128)S(1)} %collective-permute-done.9.refs_2_), channel_id=1, source_target_pairs={{0,16},{16,0},{1,17},{17,1},{2,18},{18,2},{3,19},{19,3},{4,20},{20... | collective-permute-start | bytes 393224 | tf_op jit(solution)/shard_map/ppermute | solution.py:286
  44.0 2.6 %collective-permute-start.15 = (f32[8,32,128]{2,1,0:T(8,128)S(1)}, f32[8,32,128]{2,1,0:T(8,128)S(1)}, u32[]{:S(2)}, u32[]{:S(2)}) collective-permute-start(f32[8,32,128]{2,1,0:T(8,128)S(1)} %get-tuple-element.77), channel_id=1, source_target_pairs={{0,16},{16,0},{1,17},{17,1},{2,18},{18,2},{3,19},{19,3},{4,20},{20... | collective-permute-start | bytes 393224 | tf_op jit(solution)/shard_map/ppermute | solution.py:286
  44.5 4.8 %collective-permute-start.21 = (f32[8,32,128]{2,1,0:T(8,128)S(1)}, f32[8,32,128]{2,1,0:T(8,128)S(1)}, u32[]{:S(2)}, u32[]{:S(2)}) collective-permute-start(f32[8,32,128]{2,1,0:T(8,128)S(1)} %shard_map.85), channel_id=1, source_target_pairs={{0,96},{32,0},{64,32},{96,64},{1,97},{33,1},{65,33},{97,65},{2,98}... | collective-permute-start | bytes 393224 | tf_op jit(solution)/shard_map/ppermute | solution.py:286
  45.7 6.2 %collective-permute-start.19 = (f32[8,32,128]{2,1,0:T(8,128)S(1)}, f32[8,32,128]{2,1,0:T(8,128)S(1)}, u32[]{:S(2)}, u32[]{:S(2)}) collective-permute-start(f32[8,32,128]{2,1,0:T(8,128)S(1)} %shard_map.84), channel_id=1, source_target_pairs={{0,64},{32,96},{64,0},{96,32},{1,65},{33,97},{65,1},{97,33},{2,66}... | collective-permute-start | bytes 393224 | tf_op jit(solution)/shard_map/ppermute | solution.py:286
  45.9 9.3 %collective-permute-start.17 = (f32[8,32,128]{2,1,0:T(8,128)S(1)}, f32[8,32,128]{2,1,0:T(8,128)S(1)}, u32[]{:S(2)}, u32[]{:S(2)}) collective-permute-start(f32[8,32,128]{2,1,0:T(8,128)S(1)} %shard_map.83), channel_id=1, source_target_pairs={{0,32},{32,64},{64,96},{96,0},{1,33},{33,65},{65,97},{97,1},{2,34}... | collective-permute-start | bytes 393224 | tf_op jit(solution)/shard_map/ppermute | solution.py:286
  55.3 4.5 %collective-permute-start.22 = (f32[8,32,128]{2,1,0:T(8,128)S(1)}, f32[8,32,128]{2,1,0:T(8,128)S(1)}, u32[]{:S(2)}, u32[]{:S(2)}) collective-permute-start(f32[8,32,128]{2,1,0:T(8,128)S(1)} %get-tuple-element.84.refs_0_), channel_id=1, source_target_pairs={{0,96},{32,0},{64,32},{96,64},{1,97},{33,1},{65,33},{97,65},{2,98}... | collective-permute-start | bytes 393224 | tf_op jit(solution)/shard_map/ppermute | solution.py:286
  55.4 7.0 %collective-permute-start.23 = (f32[8,32,128]{2,1,0:T(8,128)S(1)}, f32[8,32,128]{2,1,0:T(8,128)S(1)}, u32[]{:S(2)}, u32[]{:S(2)}) collective-permute-start(f32[8,32,128]{2,1,0:T(8,128)S(1)} %get-tuple-element.84.refs_0_), channel_id=1, source_target_pairs={{0,64},{32,96},{64,0},{96,32},{1,65},{33,97},{65,1},{97,33},{2,66}... | collective-permute-start | bytes 393224 | tf_op jit(solution)/shard_map/ppermute | solution.py:286
  55.6 9.1 %collective-permute-start.24 = (f32[8,32,128]{2,1,0:T(8,128)S(1)}, f32[8,32,128]{2,1,0:T(8,128)S(1)}, u32[]{:S(2)}, u32[]{:S(2)}) collective-permute-start(f32[8,32,128]{2,1,0:T(8,128)S(1)} %get-tuple-element.84.refs_0_), channel_id=1, source_target_pairs={{0,32},{32,64},{64,96},{96,0},{1,33},{33,65},{65,97},{97,1},{2,34}... | collective-permute-start | bytes 393224 | tf_op jit(solution)/shard_map/ppermute | solution.py:286
  56.8 8.9 %collective-permute-start.25 = (f32[8,32,128]{2,1,0:T(8,128)S(1)}, f32[8,32,128]{2,1,0:T(8,128)S(1)}, u32[]{:S(2)}, u32[]{:S(2)}) collective-permute-start(f32[8,32,128]{2,1,0:T(8,128)S(1)} %get-tuple-element.84.refs_0_), channel_id=1, source_target_pairs={{0,16},{16,0},{1,17},{17,1},{2,18},{18,2},{3,19},{19,3},{4,20},{20... | collective-permute-start | bytes 393224 | tf_op jit(solution)/shard_map/ppermute | solution.py:286
  59.7 5.9 %collective-permute-start.26 = (f32[8,32,128]{2,1,0:T(8,128)S(1)}, f32[8,32,128]{2,1,0:T(8,128)S(1)}, u32[]{:S(2)}, u32[]{:S(2)}) collective-permute-start(f32[8,32,128]{2,1,0:T(8,128)S(1)} %collective-permute-done.22.refs_1_), channel_id=1, source_target_pairs={{0,16},{16,0},{1,17},{17,1},{2,18},{18,2},{3,19},{19,3},{4,20},{20... | collective-permute-start | bytes 393224 | tf_op jit(solution)/shard_map/ppermute | solution.py:286
  62.4 3.3 %collective-permute-start.27 = (f32[8,32,128]{2,1,0:T(8,128)S(1)}, f32[8,32,128]{2,1,0:T(8,128)S(1)}, u32[]{:S(2)}, u32[]{:S(2)}) collective-permute-start(f32[8,32,128]{2,1,0:T(8,128)S(1)} %collective-permute-done.23.refs_2_), channel_id=1, source_target_pairs={{0,16},{16,0},{1,17},{17,1},{2,18},{18,2},{3,19},{19,3},{4,20},{20... | collective-permute-start | bytes 393224 | tf_op jit(solution)/shard_map/ppermute | solution.py:286
  73.8 3.9 %collective-permute-start.29 = (f32[8,32,128]{2,1,0:T(8,128)S(1)}, f32[8,32,128]{2,1,0:T(8,128)S(1)}, u32[]{:S(2)}, u32[]{:S(2)}) collective-permute-start(f32[8,32,128]{2,1,0:T(8,128)S(1)} %get-tuple-element.87), channel_id=1, source_target_pairs={{0,16},{16,0},{1,17},{17,1},{2,18},{18,2},{3,19},{19,3},{4,20},{20... | collective-permute-start | bytes 393224 | tf_op jit(solution)/shard_map/ppermute | solution.py:286
  74.3 7.4 %collective-permute-start.35 = (f32[8,32,128]{2,1,0:T(8,128)S(1)}, f32[8,32,128]{2,1,0:T(8,128)S(1)}, u32[]{:S(2)}, u32[]{:S(2)}) collective-permute-start(f32[8,32,128]{2,1,0:T(8,128)S(1)} %shard_map.90), channel_id=1, source_target_pairs={{0,96},{32,0},{64,32},{96,64},{1,97},{33,1},{65,33},{97,65},{2,98}... | collective-permute-start | bytes 393224 | tf_op jit(solution)/shard_map/ppermute | solution.py:286
  75.5 7.5 %collective-permute-start.33 = (f32[8,32,128]{2,1,0:T(8,128)S(1)}, f32[8,32,128]{2,1,0:T(8,128)S(1)}, u32[]{:S(2)}, u32[]{:S(2)}) collective-permute-start(f32[8,32,128]{2,1,0:T(8,128)S(1)} %shard_map.89), channel_id=1, source_target_pairs={{0,64},{32,96},{64,0},{96,32},{1,65},{33,97},{65,1},{97,33},{2,66}... | collective-permute-start | bytes 393224 | tf_op jit(solution)/shard_map/ppermute | solution.py:286
  75.7 11.4 %collective-permute-start.31 = (f32[8,32,128]{2,1,0:T(8,128)S(1)}, f32[8,32,128]{2,1,0:T(8,128)S(1)}, u32[]{:S(2)}, u32[]{:S(2)}) collective-permute-start(f32[8,32,128]{2,1,0:T(8,128)S(1)} %shard_map.88), channel_id=1, source_target_pairs={{0,32},{32,64},{64,96},{96,0},{1,33},{33,65},{65,97},{97,1},{2,34}... | collective-permute-start | bytes 393224 | tf_op jit(solution)/shard_map/ppermute | solution.py:286
  76.4 39.7 %collective-permute-start.37 = (f32[8,4096]{1,0:T(8,128)S(1)}, f32[8,4096]{1,0:T(8,128)S(1)}, u32[]{:S(2)}, u32[]{:S(2)}) collective-permute-start(f32[8,4096]{1,0:T(8,128)S(1)} %get-tuple-element.107), channel_id=1, source_target_pairs={{1,0},{2,1},{3,2},{4,3},{5,4},{6,5},{7,6},{8,7},{9,8},{10,9},{11,1... | collective-permute-start | bytes 393224 | tf_op jit(solution)/shard_map/ppermute | solution.py:346
  77.7 38.4 %collective-permute-start.38 = (f32[8,4096]{1,0:T(8,128)S(1)}, f32[8,4096]{1,0:T(8,128)S(1)}, u32[]{:S(2)}, u32[]{:S(2)}) collective-permute-start(f32[8,4096]{1,0:T(8,128)S(1)} %get-tuple-element.106), channel_id=1, source_target_pairs={{0,1},{1,2},{2,3},{3,4},{4,5},{5,6},{6,7},{7,8},{8,9},{9,10},{10,1... | collective-permute-start | bytes 393224 | tf_op jit(solution)/shard_map/ppermute | solution.py:345
  81.7 34.4 %collective-permute-start.39 = (f32[32,8,128]{2,1,0:T(8,128)S(1)}, f32[32,8,128]{2,1,0:T(8,128)S(1)}, u32[]{:S(2)}, u32[]{:S(2)}) collective-permute-start(f32[32,8,128]{2,1,0:T(8,128)S(1)} %get-tuple-element.103), channel_id=1, source_target_pairs={{1,0},{2,1},{3,2},{4,3},{5,4},{6,5},{7,6},{8,7},{9,8},{10,9},{11,1... | collective-permute-start | bytes 393224 | tf_op jit(solution)/shard_map/ppermute | solution.py:365
  83.0 33.1 %collective-permute-start.40 = (f32[32,8,128]{2,1,0:T(8,128)S(1)}, f32[32,8,128]{2,1,0:T(8,128)S(1)}, u32[]{:S(2)}, u32[]{:S(2)}) collective-permute-start(f32[32,8,128]{2,1,0:T(8,128)S(1)} %get-tuple-element.104), channel_id=1, source_target_pairs={{0,1},{1,2},{2,3},{3,4},{4,5},{5,6},{6,7},{7,8},{8,9},{9,10},{10,1... | collective-permute-start | bytes 393224 | tf_op jit(solution)/shard_map/ppermute | solution.py:364
  87.2 2.9 %collective-permute-start.36 = (f32[8,128]{1,0:T(8,128)S(1)}, f32[8,128]{1,0:T(8,128)S(1)}, u32[]{:S(2)}, u32[]{:S(2)}) collective-permute-start(f32[8,128]{1,0:T(8,128)S(1)} %get-tuple-element.98.own), channel_id=1, source_target_pairs={{0,16},{16,0},{1,17},{17,1},{2,18},{18,2},{3,19},{19,3},{4,20},{20... | collective-permute-start | bytes 12296 | tf_op jit(solution)/shard_map/ppermute | solution.py:286
  90.8 23.9 %all-to-all-start.1 = ((f32[64,1,128]{2,1,0:T(1,128)}), f32[64,1,128]{2,1,0:T(1,128)S(1)}, u32[]{:S(2)}, u32[]{:S(2)}) async-start(f32[64,1,128]{2,1,0:T(1,128)} %bitcast.9), calls=%async_computation.1 | async-start | bytes 65536 | tf_op jit(solution)/shard_map/all_to_all | solution.py:312
  (16 other events, 105.9 us)
